TPU v7x, 128 devices: a whole 4x4x4 slice. The times are simulated.
128 devices in a mesh: seq: 64 (over z, y_hi, x, core), tp: 2 (over y_lo).
Axes of the slice: x: 4, y: 4 (y_hi: 2, y_lo: 2; y = y_hi * 2 + y_lo), z: 4, core: 2. Of those that a mesh axis runs over, the one named last changes fastest.
Arguments:
- mixer_input: bfloat16 [32768, 3072], P('seq', 'tp'), may hold values from -6 to 6
- state_write: bfloat16 [32768, 128], P('seq'), may hold values from -2 to 2
- state_read: bfloat16 [32768, 128], P('seq'), may hold values from -2 to 2
- step_size: float32 [32768, 48], P('seq', 'tp'), may hold values from 0.05 to 0.5
- log_decay: float32 [32768, 48], P('seq', 'tp'), may hold values from -1.8 to 0, as said below
- skip_gain: float32 [48], P('tp'), may hold values from 0.5 to 2
- head_gain: float32 [3072], P('tp'), may hold values from 0.25 to 1.75
- mixer_out: bfloat16 [3072, 3072], P('tp'), may hold values from -0.109375 to 0.109375
- residual: bfloat16 [32768, 3072], P('seq', 'tp'), may hold values from -6 to 6
- attn_gain: float32 [3072], replicated, may hold values from 0.25 to 1.75
- qkv_weight: bfloat16 [3072, 3, 1536], P(None, None, 'tp'), may hold values from -2 to 2
Outputs:
- stream: bfloat16 [32768, 3072], P('seq', 'tp')
- attended: bfloat16 [32768, 1536], P('seq', 'tp')
Inputs may be any that keep to these rules, and one draw needn't show every extreme that they name: `log_decay`: negative everywhere.
All inputs are finite; a program needn't handle non-finite values.
Results may differ from a plain program's by a relative error of at most 0.03.
Values may be sent and summed in bfloat16 or wider, within the bound.
A program may use at most 192 MiB of HBM per device.

v0:
```python
import jax
import jax.numpy as jnp
from jax import lax
from jax.sharding import Mesh
from jax.sharding import PartitionSpec as P

AHD = 96
WINDOW = 2048
SEQ = ("seq_0", "seq_1", "seq_2", "seq_3")


EPSILON = 1e-05


def filled_with(x, identity):
    return jax.tree.map(
        lambda a, e: jnp.broadcast_to(jnp.asarray(e, a.dtype), a.shape), x, identity
    )


def carried_in(x, axes, combine, identity):
    before = start = filled_with(x, identity)
    running = x
    for axis in reversed(axes):
        size, position = (lax.axis_size(axis), lax.axis_index(axis))
        pieces = jax.tree.map(
            lambda part, kind: lax.all_gather(part.astype(kind), axis),
            running,
            jax.tree.map(lambda a: jnp.bfloat16 if a.dtype == jnp.float32 else a.dtype, x),
        )
        inside, running = (start, start)
        for k in range(size):
            passed = k < position
            running = combine(
                running, jax.tree.map(lambda part, own: part[k].astype(own.dtype), pieces, x)
            )
            inside = jax.tree.map(lambda new, old: jnp.where(passed, new, old), running, inside)
        before = combine(inside, before)
    return before


def split_up(x, dim, size):
    lengths = x.shape
    pieces = x.reshape(*lengths[:dim], size, lengths[dim] // size, *lengths[dim + 1 :])
    return jnp.moveaxis(pieces, dim, 0)


def sum_at_owner(x, axis, dim):
    pieces = split_up(x, dim, lax.axis_size(axis))
    arrived = lax.all_to_all(pieces, axis, split_axis=0, concat_axis=0, tiled=True)
    return arrived.astype(jnp.float32).sum(axis=0)


def from_everyone(x, axis):
    size = lax.axis_size(axis)
    return lax.all_to_all(jnp.broadcast_to(x[None], (size, *x.shape)), axis, 0, 0, tiled=True)


def over_copies(x, axis):
    everything = from_everyone(x, axis)
    return jnp.sum(everything, axis=0)


def joined_along(pieces, dim):
    pieces = jnp.moveaxis(pieces, 0, dim)
    lengths = pieces.shape
    return pieces.reshape(*lengths[:dim], lengths[dim] * lengths[dim + 1], *lengths[dim + 2 :])


def gathered_copies(x, axis, dim):
    return joined_along(from_everyone(x, axis), dim)


def shifted(x, axis, by):
    size = lax.axis_size(axis)
    pairs = [(i, i + by) for i in range(size) if 0 <= i + by < size]
    return lax.ppermute(x, axis, pairs)


def span_terms(inputs, write_rows, read_rows, step_rows, decays, skip_gain):
    length, head_count = step_rows.shape
    head_dim = inputs.shape[1] // head_count
    cumulative = jnp.cumsum(decays, axis=0)
    totals = cumulative[-1]
    values = inputs.astype(jnp.float32).reshape(length, head_count, head_dim)
    scaled = (step_rows[:, :, None] * values).astype(jnp.bfloat16)
    intersection = jnp.dot(read_rows, write_rows.T, preferred_element_type=jnp.float32)
    sequence_place = jnp.arange(length)
    causal = sequence_place[:, None] >= sequence_place[None, :]
    log_gaps = cumulative.T[:, :, None] - cumulative.T[:, None, :]
    mixing = (
        jnp.where(causal, jnp.exp(jnp.where(causal, log_gaps, 0.0)), 0.0) * intersection
    ).astype(jnp.bfloat16)
    inner_part = jnp.einsum("hts,shp->thp", mixing, scaled, preferred_element_type=jnp.float32)
    local_part = inner_part + skip_gain[None, :, None] * values
    written = jnp.exp(totals[None, :] - cumulative)[:, :, None] * scaled.astype(jnp.float32)
    state_term = jnp.einsum(
        "shp,sn->hpn", written, write_rows.astype(jnp.float32), precision=lax.Precision.HIGHEST
    )
    return (local_part, state_term, totals, cumulative)


def join_states(earlier_pair, later_pair):
    return (
        earlier_pair[0] * later_pair[0],
        later_pair[0][:, None, None] * earlier_pair[1] + later_pair[1],
    )


def fold_spans(running, span_piece):
    state_term, totals = span_piece
    decay_run, state_run = running
    factor = jnp.exp(totals)
    return (
        (decay_run * factor, factor[:, None, None] * state_run + state_term),
        (decay_run, state_run),
    )


def on_device(
    mixer_input,
    state_write,
    state_read,
    step_size,
    log_decay,
    skip_gain,
    head_gain,
    mixer_out,
    residual,
    attn_gain,
    qkv_weight,
):
    tokens_dev = mixer_input.shape[0]
    head_count = step_size.shape[1]
    channels = mixer_input.shape[1]
    head_dim = channels // head_count
    span_len = min(tokens_dev, 256)
    span_count = tokens_dev // span_len

    def blocked(tensor):
        return tensor.reshape((span_count, span_len) + tensor.shape[1:])

    local_part, state_terms, totals, cumulative = jax.vmap(
        span_terms, in_axes=(0, 0, 0, 0, 0, None)
    )(
        blocked(mixer_input),
        blocked(state_write),
        blocked(state_read),
        blocked(step_size),
        blocked(log_decay),
        skip_gain,
    )
    identity_pair = (
        jnp.ones((head_count,), jnp.float32),
        jnp.zeros((head_count, head_dim, state_write.shape[1]), jnp.float32),
    )
    device_pair, before = lax.scan(fold_spans, identity_pair, (state_terms, totals))
    carry_in = carried_in(device_pair, SEQ, join_states, identity_pair)
    entering = before[0][:, :, None, None] * carry_in[1][None] + before[1]
    from_before = jnp.exp(cumulative)[..., None] * jnp.einsum(
        "ctn,chpn->cthp",
        blocked(state_read).astype(jnp.float32),
        entering,
        precision=lax.Precision.HIGHEST,
    )
    head_outputs = (local_part + from_before).reshape(tokens_dev, head_count, head_dim)
    inverse_rms = lax.rsqrt(jnp.mean(head_outputs * head_outputs, axis=2, keepdims=True) + EPSILON)
    normed = ((head_outputs * inverse_rms).reshape(tokens_dev, channels) * head_gain).astype(
        jnp.bfloat16
    )
    partial_value = jnp.dot(normed, mixer_out, preferred_element_type=jnp.float32)
    model_width = partial_value.shape[1]
    half_width = residual.shape[1]
    own_sum = sum_at_owner(partial_value.astype(jnp.bfloat16), "tp", 1)
    stream = (residual.astype(jnp.float32) + own_sum).astype(jnp.bfloat16)
    stream_wide = stream.astype(jnp.float32)
    squares = over_copies(jnp.sum(stream_wide * stream_wide, axis=1), "tp")
    gain_half = lax.dynamic_slice_in_dim(
        attn_gain, lax.axis_index("tp") * half_width, half_width, 0
    )
    normed_half = (
        stream_wide * lax.rsqrt(squares / model_width + EPSILON)[:, None] * gain_half
    ).astype(jnp.bfloat16)
    normed_stream = gathered_copies(normed_half, "tp", 1)
    projected = jnp.dot(
        normed_stream, qkv_weight.reshape(model_width, -1), preferred_element_type=jnp.float32
    ).astype(jnp.bfloat16)
    embed_dev = qkv_weight.shape[2]
    query_all = projected[:, :embed_dev]
    key_value = projected[:, embed_dev:]
    reach_blocks = WINDOW // tokens_dev
    gathered_count = 0
    collected = key_value
    while gathered_count < reach_blocks:
        distance = 1 if gathered_count == 0 else gathered_count
        arrived = shifted(collected, SEQ, distance)
        collected = (
            arrived if gathered_count == 0 else jnp.concatenate([arrived, collected], axis=0)
        )
        gathered_count = 1 if gathered_count == 0 else 2 * gathered_count
    context = jnp.concatenate([collected, key_value], axis=0)
    attn_heads = embed_dev // AHD
    first_valid = WINDOW - lax.axis_index(SEQ) * tokens_dev
    query_block = min(tokens_dev, 512)
    queries = query_all.reshape(query_block, attn_heads, AHD)
    key_part = context[:, :embed_dev].reshape(-1, attn_heads, AHD)
    value_part = context[:, embed_dev:].reshape(-1, attn_heads, AHD)
    scores = jnp.einsum(
        "thd,rhd->htr", queries, key_part, preferred_element_type=jnp.float32
    ) * AHD ** (-0.5)
    query_pos = 0 + jnp.arange(query_block)
    key_pos = 0 + jnp.arange(context.shape[0])
    allowed = (
        (key_pos[None, :] > query_pos[:, None])
        & (key_pos[None, :] <= query_pos[:, None] + WINDOW)
        & (key_pos[None, :] >= first_valid)
    )
    masked = jnp.where(allowed[None], scores, -jnp.inf)
    peak = jnp.max(masked, axis=2, keepdims=True)
    raised = jnp.exp(masked - peak)
    weights = (raised / jnp.sum(raised, axis=2, keepdims=True)).astype(jnp.bfloat16)
    result = jnp.einsum("htr,rhd->thd", weights, value_part, preferred_element_type=jnp.float32)
    pieces = result.astype(jnp.bfloat16).reshape(query_block, embed_dev)
    return (stream, pieces)


def solution(mesh):
    torus = Mesh(
        mesh.devices.reshape(4, 2, 4, 2, mesh.shape["tp"]),
        ("seq_0", "seq_1", "seq_2", "seq_3", "tp"),
    )
    in_specs = (
        P(SEQ, "tp"),
        P(SEQ, None),
        P(SEQ, None),
        P(SEQ, "tp"),
        P(SEQ, "tp"),
        P("tp"),
        P("tp"),
        P("tp", None),
        P(SEQ, "tp"),
        P(),
        P(None, None, "tp"),
    )
    out_specs = (P(SEQ, "tp"), P(SEQ, "tp"))
    return jax.shard_map(
        on_device, mesh=torus, in_specs=in_specs, out_specs=out_specs, check_vma=False
    )
```

profile of v0, /device:TPU:32, one launch (start us, length us, event | category | flops | bytes accessed | tf_op | source)
XLA Modules:
  0.0 430.8 jit_solution(2144466407367607810)
XLA Ops:
  11.8 5.2 %reshape.417 = f32[2,256,24,64]{3,2,1,0:T(8,128)} reshape(bf16[512,1536]{1,0:T(8,128)(2,1)} %param.13) | data formatting | bytes 4718592 | tf_op jit(solution)/shard_map/vmap()/convert_element_type | solution.py:85
  17.0 6.2 %copy.122 = f32[2,256,24,64]{1,3,2,0:T(8,128)} copy(f32[2,256,24,64]{3,2,1,0:T(8,128)} %reshape.417) | data formatting | bytes 6291456 | tf_op jit(solution)/shard_map/vmap()/convert_element_type | solution.py:85
  33.3 9.7 %all-gather.2 = bf16[4,1,24]{2,1,0:T(2,128)(2,1)S(1)} all-gather(bf16[1,1,24]{2,1,0:T(2,128)(2,1)S(1)} %convert_bitcast_fusion), channel_id=1, replica_groups=mesh['seq_0'=4,'seq_1'=2,'seq_2'=4,'seq_3'=2,'tp'=2] {'seq_2'}, dimensions={0}, use_global_device_ids=true | all-gather | bytes 240 | tf_op jit(solution)/shard_map/all_gather | solution.py:27
  43.0 5.7 %all-gather.3 = bf16[2,1,24]{2,1,0:T(2,128)(2,1)S(1)} all-gather(bf16[1,1,24]{2,1,0:T(2,128)(2,1)S(1)} %fusion.52), channel_id=1, replica_groups=mesh['seq_0'=4,'seq_1'=2,'seq_2'=4,'seq_3'=2,'tp'=2] {'seq_1'}, dimensions={0}, use_global_device_ids=true | all-gather | bytes 144 | tf_op jit(solution)/shard_map/all_gather | solution.py:27
  53.0 26.3 %all-gather.8.cloned.1.call-done = bf16[4,24,64,128]{3,2,1,0:T(8,128)(2,1)} async-done(((bf16[1,24,64,128]{3,2,1,0:T(8,128)(2,1)}), bf16[4,24,64,128]{3,2,1,0:T(8,128)(2,1)}) %all-gather.8.cloned.1.call-update) | async-done | bytes 1572880 | tf_op jit(solution)/shard_map/all_gather | solution.py:27
  81.2 12.9 %all_gather.44 = bf16[2,24,64,128]{3,2,1,0:T(8,128)(2,1)S(1)} all-gather(bf16[1,24,64,128]{3,2,1,0:T(8,128)(2,1)S(1)} %fusion.41), channel_id=1, replica_groups=mesh['seq_0'=4,'seq_1'=2,'seq_2'=4,'seq_3'=2,'tp'=2] {'seq_1'}, dimensions={0}, use_global_device_ids=true | all-gather | bytes 1179648 | tf_op jit(solution)/shard_map/all_gather | solution.py:27
  95.2 8.1 %all-gather.4 = bf16[4,1,24]{2,1,0:T(2,128)(2,1)S(1)} all-gather(bf16[1,1,24]{2,1,0:T(2,128)(2,1)S(1)} %multiply_convert_fusion.7), channel_id=1, replica_groups=mesh['seq_0'=4,'seq_1'=2,'seq_2'=4,'seq_3'=2,'tp'=2] {'seq_0'}, dimensions={0}, use_global_device_ids=true | all-gather | bytes 240 | tf_op jit(solution)/shard_map/all_gather | solution.py:27
  105.5 15.2 %all-gather.10.cloned.1.call-done = bf16[4,24,64,128]{3,2,1,0:T(8,128)(2,1)} async-done(((bf16[1,24,64,128]{3,2,1,0:T(8,128)(2,1)}), bf16[4,24,64,128]{3,2,1,0:T(8,128)(2,1)}) %all-gather.10.cloned.1.call-update) | async-done | bytes 1572880 | tf_op jit(solution)/shard_map/all_gather | solution.py:27
  120.7 3.7 fusion.38
  126.4 4.0 multiply_reduce_fusion
  135.2 5.4 %convolution_convert_fusion.1 = bf16[512,3072]{1,0:T(8,128)(2,1)S(1)} fusion(bf16[512,1536]{0,1:T(8,128)(2,1)S(1)} %fusion.22, bf16[1536,3072]{1,0:T(8,128)(2,1)S(1)} %bitcast.201), kind=kOutput, calls=%fused_computation.31 | convolution fusion | flops 4833411072 | bytes 14155776 | tf_op jit(solution)/shard_map/dot_general | solution.py:171
  140.8 38.7 %all_to_all.16 = bf16[2,512,1536]{2,1,0:T(8,128)(2,1)S(1)} all-to-all(bf16[2,512,1536]{2,1,0:T(8,128)(2,1)S(1)} %bitcast.186), channel_id=1, replica_groups=mesh['seq_0'=4,'seq_1'=2,'seq_2'=4,'seq_3'=2,'tp'=2] {'tp'}, dimensions={0} | all-to-all | bytes 6291456 | tf_op jit(solution)/shard_map/all_to_all | solution.py:50
  185.4 3.7 all-to-all-done.1
  192.1 3.9 all-to-all-start.2
  196.1 18.6 %copy.132 = bf16[3072,3,768]{0,2,1:T(8,128)(2,1)} copy(bf16[3072,3,768]{2,0,1:T(8,128)(2,1)} %param.23) | data formatting | bytes 28311552 | tf_op args[10]
  214.7 15.4 %all-to-all-done.2 = bf16[2,512,1536]{1,2,0:T(8,128)(2,1)S(1)} async-done(((bf16[2,512,1536]{1,2,0:T(8,128)(2,1)}), bf16[2,512,1536]{1,2,0:T(8,128)(2,1)S(1)}, u32[]{:S(2)}, u32[]{:S(2)}) %all-to-all-start.2) | async-done | bytes 3145760 | tf_op jit(solution)/shard_map/all_to_all | solution.py:56
  230.1 11.6 %convolution_convert_fusion = bf16[512,2304]{1,0:T(8,128)(2,1)S(1)} fusion(bf16[512,3072]{0,1:T(8,128)(2,1)S(1)} %bitcast.189, bf16[3072,2304]{0,1:T(8,128)(2,1)} %bitcast.183), kind=kOutput, calls=%fused_computation.30 | convolution fusion | flops 7248936960 | bytes 19660800 | tf_op jit(solution)/shard_map/dot_general | solution.py:185
  243.7 24.3 %collective-permute-done = bf16[512,1536]{1,0:T(8,128)(2,1)S(1)} collective-permute-done((bf16[512,1536]{1,0:T(8,128)(2,1)S(1)}, bf16[512,1536]{1,0:T(8,128)(2,1)S(1)}, u32[]{:S(2)}, u32[]{:S(2)}) %collective-permute-start) | collective-permute-done | bytes 1572896 | tf_op jit(solution)/shard_map/ppermute | solution.py:77
  270.0 24.3 %collective-permute-done.1 = bf16[512,1536]{1,0:T(8,128)(2,1)S(1)} collective-permute-done((bf16[512,1536]{1,0:T(8,128)(2,1)S(1)}, bf16[512,1536]{1,0:T(8,128)(2,1)S(1)}, u32[]{:S(2)}, u32[]{:S(2)}) %collective-permute-start.1) | collective-permute-done | bytes 1572896 | tf_op jit(solution)/shard_map/ppermute | solution.py:77
  305.3 61.4 %collective-permute-done.2 = bf16[1024,1536]{1,0:T(8,128)(2,1)} collective-permute-done((bf16[1024,1536]{1,0:T(8,128)(2,1)}, bf16[1024,1536]{1,0:T(8,128)(2,1)}, u32[]{:S(2)}, u32[]{:S(2)}) %collective-permute-start.2) | collective-permute-done | bytes 3145760 | tf_op jit(solution)/shard_map/ppermute | solution.py:77
  373.4 6.3 %copy.135 = bf16[2560,768]{0,1:T(8,128)(2,1)} copy(bf16[2560,768]{1,0:T(8,128)(2,1)} %get-tuple-element.108) | data formatting | bytes 7864320 | tf_op jit(solution)/shard_map/slice | solution.py:206
  379.7 6.4 %copy.133 = bf16[2560,768]{0,1:T(8,128)(2,1)} copy(bf16[2560,768]{1,0:T(8,128)(2,1)} %get-tuple-element.109) | data formatting | bytes 7864320 | tf_op jit(solution)/shard_map/slice | solution.py:207
  386.1 20.4 %fusion.66 = (f32[8,512]{1,0:T(8,128)S(1)}, f32[8,512,2560]{2,1,0:T(8,128)}) fusion(pred[512,2560]{1,0:T(8,128)(4,1)S(1)} %copy-done.9, bf16[512,8,96]{0,2,1:T(8,128)(2,1)S(1)} %bitcast.191, bf16[2560,8,96]{0,2,1:T(8,128)(2,1)} %bitcast.187), kind=kOutput, calls=%fused_computation.139 | convolution fusion | flops 2055211520 | bytes 47988736 | tf_op jit(solution)/shard_map/sub | solution.py:220
  406.5 16.3 %fusion.31 = bf16[8,96,512]{2,1,0:T(8,128)(2,1)S(1)} fusion(bf16[2560,8,96]{0,2,1:T(8,128)(2,1)} %bitcast.188, f32[8,512,2560]{2,1,0:T(8,128)} %get-tuple-element.126, f32[8,512]{1,0:T(8,128)S(1)} %get-tuple-element.125), kind=kOutput, calls=%fused_computation.55 | convolution fusion | flops 2034630656 | bytes 46678016 | tf_op jit(solution)/shard_map/htr,rhd->thd/dot_general | solution.py:222
  (127 shorter events, 64.1 us)
Async XLA Ops:
  7.2 97.3 %copy-start = (bf16[512,128]{1,0:T(8,128)(2,1)S(1)}, bf16[512,128]{1,0:T(8,128)(2,1)}, u32[]{:S(2)}) copy-start(bf16[512,128]{1,0:T(8,128)(2,1)} %param.15) | copy-start | bytes 393220
  7.2 72.1 %all-gather.8.cloned.1.call-start = ((), (), s32[]{:S(2)}) async-start(), calls=%async_computation.3 | async-start | bytes 1966080 | tf_op jit(solution)/shard_map/all_gather | solution.py:27
  17.0 6.2 %copy-start.12 = (bf16[512,128]{1,0:T(8,128)(2,1)S(1)}, bf16[512,128]{1,0:T(8,128)(2,1)}, u32[]{:S(2)}) copy-start(bf16[512,128]{1,0:T(8,128)(2,1)} %param.14) | copy-start | bytes 393220
  26.8 2.4 copy-start.20
  29.1 23.8 %copy-start.17 = (f32[2,24]{1,0:T(2,128)}, f32[2,24]{1,0:T(2,128)S(1)}, u32[]{:S(2)}) copy-start(f32[2,24]{1,0:T(2,128)S(1)} %get-tuple-element.42) | copy-start | bytes 580
  52.9 67.8 %all-gather.10.cloned.1.call-start = ((), (), s32[]{:S(2)}) async-start(), calls=%async_computation.4 | async-start | bytes 1966080 | tf_op jit(solution)/shard_map/all_gather | solution.py:27
  79.3 41.4 %copy-start.3 = (bf16[4,24,64,128]{3,2,1,0:T(8,128)(2,1)S(1)}, bf16[4,24,64,128]{3,2,1,0:T(8,128)(2,1)}, u32[]{:S(2)}) copy-start(bf16[4,24,64,128]{3,2,1,0:T(8,128)(2,1)} %all-gather.8.cloned.1.call-done) | copy-start | bytes 4718596
  105.5 19.0 %copy-start.18 = (f32[2,24]{1,0:T(2,128)S(1)}, f32[2,24]{1,0:T(2,128)}, u32[]{:S(2)}) copy-start(f32[2,24]{1,0:T(2,128)} %copy-done.17) | copy-start | bytes 580
  120.7 3.8 copy-start.8
  130.5 3.6 slice-start
  130.5 3.6 slice-start.1
  133.0 2.2 slice-start.2
  180.9 4.4 %copy-start.16 = (f32[3072]{0:T(1024)S(1)}, f32[3072]{0:T(1024)}, u32[]{:S(2)}) copy-start(f32[3072]{0:T(1024)} %param.22) | copy-start | bytes 36868
  181.5 7.7 %copy-start.4 = (bf16[512,1536]{1,0:T(8,128)(2,1)}, bf16[512,1536]{1,0:T(8,128)(2,1)S(1)}, u32[]{:S(2)}) copy-start(bf16[512,1536]{1,0:T(8,128)(2,1)S(1)} %get-tuple-element.103) | copy-start | bytes 4718596
  182.1 7.0 %all-to-all-start.1 = ((f32[2,1,512]{2,1,0:T(1,128)}), f32[2,1,512]{2,1,0:T(1,128)S(1)}, u32[]{:S(2)}, u32[]{:S(2)}) async-start(f32[2,1,512]{2,1,0:T(1,128)} %broadcast_in_dim.53), calls=%async_computation.1 | async-start | bytes 8192 | tf_op jit(solution)/shard_map/all_to_all | solution.py:56
  192.1 38.0 %all-to-all-start.2 = ((bf16[2,512,1536]{1,2,0:T(8,128)(2,1)}), bf16[2,512,1536]{1,2,0:T(8,128)(2,1)S(1)}, u32[]{:S(2)}, u32[]{:S(2)}) async-start(bf16[2,512,1536]{1,2,0:T(8,128)(2,1)} %broadcast_in_dim.54), calls=%async_computation.2 | async-start | bytes 6291456 | tf_op jit(solution)/shard_map/all_to_all | solution.py:56
  241.7 54.7 %copy-start.6 = (bf16[512,2304]{1,0:T(8,128)(2,1)}, bf16[512,2304]{1,0:T(8,128)(2,1)S(1)}, u32[]{:S(2)}) copy-start(bf16[512,2304]{1,0:T(8,128)(2,1)S(1)} %convolution_convert_fusion) | copy-start | bytes 7077892
  241.8 26.2 %collective-permute-start = (bf16[512,1536]{1,0:T(8,128)(2,1)S(1)}, bf16[512,1536]{1,0:T(8,128)(2,1)S(1)}, u32[]{:S(2)}, u32[]{:S(2)}) collective-permute-start(bf16[512,1536]{1,0:T(8,128)(2,1)S(1)} %slice.163), channel_id=1, source_target_pairs={{0,2},{2,4},{4,6},{6,8},{8,10},{10,12},{12,14},{14,16},{16,18},{18... | collective-permute-start | bytes 4718600 | tf_op jit(solution)/shard_map/ppermute | solution.py:77
  268.1 26.2 %collective-permute-start.1 = (bf16[512,1536]{1,0:T(8,128)(2,1)S(1)}, bf16[512,1536]{1,0:T(8,128)(2,1)S(1)}, u32[]{:S(2)}, u32[]{:S(2)}) collective-permute-start(bf16[512,1536]{1,0:T(8,128)(2,1)S(1)} %collective-permute-done), channel_id=1, source_target_pairs={{0,2},{2,4},{4,6},{6,8},{8,10},{10,12},{12,14},{14,16},{16,18},{18... | collective-permute-start | bytes 4718600 | tf_op jit(solution)/shard_map/ppermute | solution.py:77
  294.3 2.2 copy-start.5
  296.5 70.1 %collective-permute-start.2 = (bf16[1024,1536]{1,0:T(8,128)(2,1)}, bf16[1024,1536]{1,0:T(8,128)(2,1)}, u32[]{:S(2)}, u32[]{:S(2)}) collective-permute-start(bf16[1024,1536]{1,0:T(8,128)(2,1)} %pad_maximum_fusion.1), channel_id=1, source_target_pairs={{0,4},{2,6},{4,8},{6,10},{8,12},{10,14},{12,16},{14,18},{16,20},{1... | collective-permute-start | bytes 9437192 | tf_op jit(solution)/shard_map/ppermute | solution.py:77
  379.7 6.4 %copy-start.9 = (pred[512,2560]{1,0:T(8,128)(4,1)S(1)}, pred[512,2560]{1,0:T(8,128)(4,1)}, u32[]{:S(2)}) copy-start(pred[512,2560]{1,0:T(8,128)(4,1)} %fusion.17) | copy-start | bytes 3932164
  379.7 6.4 %copy-start.10 = (bf16[512,768]{0,1:T(8,128)(2,1)S(1)}, bf16[512,768]{0,1:T(8,128)(2,1)}, u32[]{:S(2)}) copy-start(bf16[512,768]{0,1:T(8,128)(2,1)} %copy.134) | copy-start | bytes 2359300
  406.5 17.4 %copy-start.1 = (bf16[512,128]{1,0:T(8,128)(2,1)S(1)}, bf16[512,128]{1,0:T(8,128)(2,1)}, u32[]{:S(2)}) copy-start(bf16[512,128]{1,0:T(8,128)(2,1)} %param.15) | copy-start | bytes 393220
  (7 other events, 11.9 us)
Sparse Core Ops, SparseCore 0:
  53.0 26.2 all-gather.7
  95.3 25.3 all-gather.9
where the time goes:
time: 432 us; the launch traced here: 431 us
  waiting for transfers between devices  171 us (40%)
  blocking collectives  79.9 us (18%)
  local copies, waits for them, and re-layouts  63.8 us (15%)
  matrix products  63.7 us (15%)
  other arithmetic  24.5 us (6%)
  between operations  15.3 us (4%)
  starting transfers between devices  13 us (3%)
    ppermute x3, waiting for transfers between devices, shifted(): return lax.ppermute(x, axis, pairs)  110 us
    all_gather x2, waiting for transfers between devices, carried_in(): lax.all_gather(part.astype(kind), axis)  41.5 us
    all_gather x5, blocking collectives, carried_in(): lax.all_gather(part.astype(kind), axis)  38.8 us
    all_to_all x1, blocking collectives, sum_at_owner(): lax.all_to_all(pieces, axis, split_axis=0, concat_axis=0, tiled=True)  38.7 us
    unnamed x54, local copies, waits for them, and re-layouts  23.9 us
    sub x1, matrix products, on_device(): raised = jnp.exp(masked - peak)  20.4 us
    all_to_all x2, waiting for transfers between devices, from_everyone(): lax.all_to_all(jnp.broadcast_to(x[None], (size, *x.shape)), axis, 0, 0, t...  19.1 us
    dot_general x1, matrix products, on_device(): jnp.einsum('htr,rhd->thd', weights, value_part, preferred_element_type=jn...  16.3 us
  transfers between devices with their start and end apart: 7, of which 7 were waited for; matrix products, arithmetic and copies ran while one was open for 6% of the time, Pallas kernels for 0%

commit v1 on v0

--- a/solution.py
+++ b/solution.py
@@ -2,6 +2,8 @@
 import jax.numpy as jnp
 from jax import lax
 from jax.sharding import Mesh
+from jax.experimental import pallas as pl
+from jax.experimental.pallas import tpu as pltpu
 from jax.sharding import PartitionSpec as P
 
 AHD = 96
@@ -77,6 +79,180 @@
     return lax.ppermute(x, axis, pairs)
 
 
+MESH = pl.DeviceIdType.MESH
+F32 = jnp.float32
+BF16 = jnp.bfloat16
+NEG = -1e30
+LOG2E = 1.4426950408889634
+
+
+def attn_kernel(proj_ref, out_ref, own, buf, knat, osend, oland, send_sem, recv_sem,
+                hsend_sem, hrecv_sem, osend_sem, orecv_sem):
+    z = lax.axis_index("seq_0")
+    yh = lax.axis_index("seq_1")
+    xx = lax.axis_index("seq_2")
+    cc = lax.axis_index("seq_3")
+    g = xx * 2 + cc
+    row = z * 2 + yh
+    nrow = lax.rem(row + 1, 8)
+    prow = lax.rem(row + 7, 8)
+    hd = 96
+    tok = 512
+
+    def at_group(j):
+        return {"seq_2": j // 2, "seq_3": lax.rem(j, 2)}
+
+    def at_row(r):
+        return {"seq_0": r // 2, "seq_1": lax.rem(r, 2)}
+
+    barrier = pltpu.get_barrier_semaphore()
+    for d in range(1, 8):
+        pl.semaphore_signal(barrier, inc=1, device_id=at_group(lax.rem(g + d, 8)), device_id_type=MESH)
+    pl.semaphore_signal(barrier, inc=1, device_id=at_row(nrow), device_id_type=MESH)
+    pl.semaphore_signal(barrier, inc=1, device_id=at_row(prow), device_id_type=MESH)
+    for i in range(3):
+        own[i] = proj_ref[:, i * 768:(i + 1) * 768].T
+    pl.semaphore_wait(barrier, 9)
+
+    def head(j):
+        return pl.ds(pl.multiple_of(j * hd, 32), hd)
+
+    def block_copy(d):
+        j = lax.rem(g + d, 8)
+        return pltpu.make_async_remote_copy(
+            src_ref=own.at[:, head(j), :],
+            dst_ref=buf.at[4 + g],
+            send_sem=send_sem.at[d],
+            recv_sem=recv_sem.at[g],
+            device_id=at_group(j), device_id_type=MESH)
+
+    def arrival(b):
+        return pltpu.make_async_copy(buf.at[4 + b], buf.at[4 + b], recv_sem.at[b])
+
+    def halo_copy(i):
+        return pltpu.make_async_remote_copy(
+            src_ref=buf.at[8 + i, pl.ds(1, 2)],
+            dst_ref=buf.at[i, pl.ds(1, 2)],
+            send_sem=hsend_sem.at[i],
+            recv_sem=hrecv_sem.at[i],
+            device_id=at_row(nrow), device_id_type=MESH)
+
+    for d in (4, 5, 3, 2, 6, 1, 7):
+        block_copy(d).start()
+    buf[4 + g] = own[:, head(g), :]
+
+    def arrived(b):
+        @pl.when(b != g)
+        def _():
+            arrival(b).wait()
+        knat[4 + b] = buf[4 + b, 1].T
+
+    for b in range(4, 8):
+        arrived(b)
+
+        @pl.when(row < 7)
+        def _(i=b - 4):
+            halo_copy(i).start()
+    for b in range(4):
+        arrived(b)
+
+    scale = (hd ** -0.5) * LOG2E
+    spos = lax.broadcasted_iota(jnp.int32, (tok, tok), 0)
+    tpos = lax.broadcasted_iota(jnp.int32, (tok, tok), 1)
+    causal = spos <= tpos
+
+    def one_block(step, _):
+        b = jnp.where(step < 4, 4 + step, 7 - step)
+
+        @pl.when(jnp.logical_and(step >= 4, row > 0))
+        def _():
+            halo_copy(b).wait_recv()
+            knat[b] = buf[b, 1].T
+
+        qt = buf[4 + b, 0]
+        s_diag = jnp.dot(knat[4 + b], qt, preferred_element_type=F32)
+        has_far = jnp.logical_or(step < 4, row > 0)
+        s_far = jnp.dot(knat[b], qt, preferred_element_type=F32)
+        s = jnp.where(causal, s_diag, jnp.where(has_far, s_far, NEG))
+        m = jnp.max(s, axis=0, keepdims=True)
+        p = jnp.exp2((s - m) * scale)
+        l = jnp.sum(p, axis=0, keepdims=True)
+        p_diag = jnp.where(causal, p, 0.0).astype(BF16)
+        acc = jnp.dot(buf[4 + b, 2], p_diag, preferred_element_type=F32)
+        p_far = jnp.where(causal, 0.0, p).astype(BF16)
+        v_far = jnp.where(has_far, buf[b, 2], jnp.zeros((hd, tok), BF16))
+        acc = acc + jnp.dot(v_far, p_far, preferred_element_type=F32)
+
+        def mid(j, carry):
+            m, l, acc = carry
+            s = jnp.dot(knat[j], qt, preferred_element_type=F32)
+            m_new = jnp.maximum(m, jnp.max(s, axis=0, keepdims=True))
+            alpha = jnp.exp2((m - m_new) * scale)
+            p = jnp.exp2((s - m_new) * scale)
+            l = alpha * l + jnp.sum(p, axis=0, keepdims=True)
+            acc = alpha * acc + jnp.dot(buf[j, 2], p.astype(BF16), preferred_element_type=F32)
+            return m_new, l, acc
+
+        first = jnp.where(row > 0, b + 1, jnp.maximum(b + 1, 4))
+        m, l, acc = lax.fori_loop(first, b + 4, mid, (m, l, acc))
+        osend[b] = (acc / l).astype(BF16)
+
+        @pl.when(b != g)
+        def _():
+            out_copy(b).start()
+        return 0
+
+    def out_copy(b):
+        return pltpu.make_async_remote_copy(
+            src_ref=osend.at[b],
+            dst_ref=oland.at[g],
+            send_sem=osend_sem.at[b],
+            recv_sem=orecv_sem.at[g],
+            device_id=at_group(b), device_id_type=MESH)
+
+    @pl.when(row == 0)
+    def _():
+        for i in range(4):
+            knat[i] = jnp.zeros((tok, hd), BF16)
+    lax.fori_loop(0, 8, one_block, 0)
+    oland[g] = osend[g]
+    for b in range(8):
+        @pl.when(b != g)
+        def _(b=b):
+            pltpu.make_async_copy(oland.at[b], oland.at[b], orecv_sem.at[b]).wait()
+    out_ref[...] = oland[...].reshape(8 * hd, tok).T
+    for d in range(1, 8):
+        block_copy(d).wait_send()
+    for b in range(8):
+        @pl.when(b != g)
+        def _(b=b):
+            out_copy(b).wait_send()
+
+    @pl.when(row < 7)
+    def _():
+        for i in range(4):
+            halo_copy(i).wait_send()
+
+
+def attention(proj):
+    V = pltpu.VMEM
+    D = pltpu.SemaphoreType.DMA
+    return pl.pallas_call(
+        attn_kernel,
+        name="attn",
+        out_shape=jax.ShapeDtypeStruct((512, 768), BF16),
+        in_specs=[pl.BlockSpec(memory_space=V)],
+        out_specs=pl.BlockSpec(memory_space=V),
+        scratch_shapes=[
+            V((3, 768, 512), BF16), V((12, 3, 96, 512), BF16), V((12, 512, 96), BF16),
+            V((8, 96, 512), BF16), V((8, 96, 512), BF16),
+            D((8,)), D((8,)), D((4,)), D((4,)), D((8,)), D((8,)),
+        ],
+        compiler_params=pltpu.CompilerParams(
+            collective_id=3, has_side_effects=True, vmem_limit_bytes=56 * 2**20),
+    )(proj)
+
+
 def span_terms(inputs, write_rows, read_rows, step_rows, decays, skip_gain):
     length, head_count = step_rows.shape
     head_dim = inputs.shape[1] // head_count
@@ -182,45 +358,12 @@
         stream_wide * lax.rsqrt(squares / model_width + EPSILON)[:, None] * gain_half
     ).astype(jnp.bfloat16)
     normed_stream = gathered_copies(normed_half, "tp", 1)
-    projected = jnp.dot(
-        normed_stream, qkv_weight.reshape(model_width, -1), preferred_element_type=jnp.float32
-    ).astype(jnp.bfloat16)
-    embed_dev = qkv_weight.shape[2]
-    query_all = projected[:, :embed_dev]
-    key_value = projected[:, embed_dev:]
-    reach_blocks = WINDOW // tokens_dev
-    gathered_count = 0
-    collected = key_value
-    while gathered_count < reach_blocks:
-        distance = 1 if gathered_count == 0 else gathered_count
-        arrived = shifted(collected, SEQ, distance)
-        collected = (
-            arrived if gathered_count == 0 else jnp.concatenate([arrived, collected], axis=0)
-        )
-        gathered_count = 1 if gathered_count == 0 else 2 * gathered_count
-    context = jnp.concatenate([collected, key_value], axis=0)
-    attn_heads = embed_dev // AHD
-    first_valid = WINDOW - lax.axis_index(SEQ) * tokens_dev
-    query_block = min(tokens_dev, 512)
-    queries = query_all.reshape(query_block, attn_heads, AHD)
-    key_part = context[:, :embed_dev].reshape(-1, attn_heads, AHD)
-    value_part = context[:, embed_dev:].reshape(-1, attn_heads, AHD)
-    scores = jnp.einsum(
-        "thd,rhd->htr", queries, key_part, preferred_element_type=jnp.float32
-    ) * AHD ** (-0.5)
-    query_pos = 0 + jnp.arange(query_block)
-    key_pos = 0 + jnp.arange(context.shape[0])
-    allowed = (
-        (key_pos[None, :] > query_pos[:, None])
-        & (key_pos[None, :] <= query_pos[:, None] + WINDOW)
-        & (key_pos[None, :] >= first_valid)
-    )
-    masked = jnp.where(allowed[None], scores, -jnp.inf)
-    peak = jnp.max(masked, axis=2, keepdims=True)
-    raised = jnp.exp(masked - peak)
-    weights = (raised / jnp.sum(raised, axis=2, keepdims=True)).astype(jnp.bfloat16)
-    result = jnp.einsum("htr,rhd->thd", weights, value_part, preferred_element_type=jnp.float32)
-    pieces = result.astype(jnp.bfloat16).reshape(query_block, embed_dev)
+    weight = jnp.transpose(qkv_weight, (1, 0, 2))
+    projected = jnp.concatenate(
+        [jnp.dot(normed_stream, weight[i], preferred_element_type=jnp.float32).astype(jnp.bfloat16) for i in range(3)],
+        axis=1,
+    )
+    pieces = attention(projected)
     return (stream, pieces)
 
 

time: 432 us -> 315 us (0.73)
  waiting for transfers between devices: 171 us -> 45.2 us
  Pallas kernels: 0 us -> 65.1 us
  local copies, waits for them, and re-layouts: 63.8 us -> 23 us
  matrix products: 63.7 us -> 26 us
  blocking collectives: 79.9 us -> 117 us
  starting transfers between devices: 13 us -> 3.3 us
  other arithmetic: 24.5 us -> 18.2 us
    ppermute x3 -> x0, waiting for transfers between devices: 110 us -> none  [shifted(): return lax.ppermute(x, axis, pairs)]
    pallas_call x0 -> x1, Pallas kernels: none -> 65.1 us  [attention(): pl.pallas_call(attn_kernel, name='attn', out_shape=jax.ShapeDtypeStruct((...]
    all_to_all x0 -> x1, blocking collectives: none -> 36.9 us  [from_everyone(): lax.all_to_all(jnp.broadcast_to(x[None], (size, *x.shape)), axis, 0, 0, t...]
    slice x7 -> x1, local copies, waits for them, and re-layouts: 20.7 us -> 0.17 us  [the longest x2 9.61 us: on_device(): key_part = context[:, :embed_dev].reshape(-1, attn_heads, AHD)]
    sub x1 -> x0, matrix products: 20.4 us -> none  [on_device(): raised = jnp.exp(masked - peak)]
    unnamed x54 -> x55, local copies, waits for them, and re-layouts: 23.9 us -> 6.03 us
    dot_general x2 -> x3, matrix products: 27.8 us -> 10.6 us  [on_device(): jnp.dot(normed_stream, weight[i], preferred_element_type=jnp.float32)]
    all_to_all x2 -> x1, waiting for transfers between devices: 19.1 us -> 3.68 us  [from_everyone(): lax.all_to_all(jnp.broadcast_to(x[None], (size, *x.shape)), axis, 0, 0, t...]
  transfers between devices with their start and end apart: 7 -> 3, of which waited for: 7 -> 3; matrix products, arithmetic and copies ran while one was open for 6% -> 1% of each run, Pallas kernels for 0% -> 0%
where the time goes in v1:
time: 315 us; the launch traced here: 313 us
  blocking collectives  117 us (37%)
  Pallas kernels  65.1 us (21%)
  waiting for transfers between devices  45.2 us (14%)
  matrix products  26 us (8%)
  local copies, waits for them, and re-layouts  23 us (7%)
  other arithmetic  18.2 us (6%)
  between operations  15.2 us (5%)
  starting transfers between devices  3.3 us (1%)
    pallas_call x1, Pallas kernels, attention(): pl.pallas_call(attn_kernel, name='attn', out_shape=jax.ShapeDtypeStruct((...  65.1 us
    all_gather x2, waiting for transfers between devices, carried_in(): lax.all_gather(part.astype(kind), axis)  41.5 us
    all_gather x5, blocking collectives, carried_in(): lax.all_gather(part.astype(kind), axis)  38.8 us
    all_to_all x1, blocking collectives, sum_at_owner(): lax.all_to_all(pieces, axis, split_axis=0, concat_axis=0, tiled=True)  38.7 us
    all_to_all x1, blocking collectives, from_everyone(): lax.all_to_all(jnp.broadcast_to(x[None], (size, *x.shape)), axis, 0, 0, t...  36.9 us
    convert_element_type x2, local copies, waits for them, and re-layouts, span_terms(): values = inputs.astype(jnp.float32).reshape(length, head_count, head_dim)  11.4 us
    dot_general x3, matrix products, on_device(): jnp.dot(normed_stream, weight[i], preferred_element_type=jnp.float32)  10.6 us
  transfers between devices with their start and end apart: 3, of which 3 were waited for; matrix products, arithmetic and copies ran while one was open for 1% of the time, Pallas kernels for 0%

profile of v1, /device:TPU:32, one launch (start us, length us, event | category | flops | bytes accessed | tf_op | source)
XLA Modules:
  0.0 312.9 jit_solution(17018290587575142303)
XLA Ops:
  11.0 5.2 %reshape.338 = f32[2,256,24,64]{3,2,1,0:T(8,128)} reshape(bf16[512,1536]{1,0:T(8,128)(2,1)} %param.13) | data formatting | bytes 4718592 | tf_op jit(solution)/shard_map/vmap()/convert_element_type | solution.py:261
  16.2 6.2 %copy.88 = f32[2,256,24,64]{1,3,2,0:T(8,128)} copy(f32[2,256,24,64]{3,2,1,0:T(8,128)} %reshape.338) | data formatting | bytes 6291456 | tf_op jit(solution)/shard_map/vmap()/convert_element_type | solution.py:261
  22.4 3.6 %fusion.19 = f32[2,24,64,128]{3,2,1,0:T(8,128)S(1)} fusion(bf16[2,256,128,1]{2,1,3,0:T(8,128)(2,1)S(1)} %bitcast.197, f32[2,256,24]{1,2,0:T(8,128)S(1)} %get-tuple-element.93, f32[2,256,24,64]{1,3,2,0:T(8,128)} %copy.88, f32[2,256,24]{1,2,0:T(8,128)S(1)} %bitcast.199), kind=kOutput, calls=%fused_computation.37 | convolution fusion | flops 1211105280 | bytes 4947968 | tf_op jit(solution)/shard_map/vmap(shp,sn->hpn)/dot_general | solution.py:273
  26.0 2.3 while.17
  29.9 2.4 all-reduce
  32.5 9.7 %all-gather.2 = bf16[4,1,24]{2,1,0:T(2,128)(2,1)S(1)} all-gather(bf16[1,1,24]{2,1,0:T(2,128)(2,1)S(1)} %convert_bitcast_fusion), channel_id=1, replica_groups=mesh['seq_0'=4,'seq_1'=2,'seq_2'=4,'seq_3'=2,'tp'=2] {'seq_2'}, dimensions={0}, use_global_device_ids=true | all-gather | bytes 240 | tf_op jit(solution)/shard_map/all_gather | solution.py:29
  42.2 5.7 %all-gather.3 = bf16[2,1,24]{2,1,0:T(2,128)(2,1)S(1)} all-gather(bf16[1,1,24]{2,1,0:T(2,128)(2,1)S(1)} %fusion.49), channel_id=1, replica_groups=mesh['seq_0'=4,'seq_1'=2,'seq_2'=4,'seq_3'=2,'tp'=2] {'seq_1'}, dimensions={0}, use_global_device_ids=true | all-gather | bytes 144 | tf_op jit(solution)/shard_map/all_gather | solution.py:29
  48.0 2.4 all-gather.1
  52.1 26.4 %all-gather.8.cloned.1.call-done = bf16[4,24,64,128]{3,2,1,0:T(8,128)(2,1)} async-done(((bf16[1,24,64,128]{3,2,1,0:T(8,128)(2,1)}), bf16[4,24,64,128]{3,2,1,0:T(8,128)(2,1)}) %all-gather.8.cloned.1.call-update) | async-done | bytes 1572880 | tf_op jit(solution)/shard_map/all_gather | solution.py:29
  80.4 12.9 %all_gather.44 = bf16[2,24,64,128]{3,2,1,0:T(8,128)(2,1)S(1)} all-gather(bf16[1,24,64,128]{3,2,1,0:T(8,128)(2,1)S(1)} %fusion.38), channel_id=1, replica_groups=mesh['seq_0'=4,'seq_1'=2,'seq_2'=4,'seq_3'=2,'tp'=2] {'seq_1'}, dimensions={0}, use_global_device_ids=true | all-gather | bytes 1179648 | tf_op jit(solution)/shard_map/all_gather | solution.py:29
  94.4 8.1 %all-gather.4 = bf16[4,1,24]{2,1,0:T(2,128)(2,1)S(1)} all-gather(bf16[1,1,24]{2,1,0:T(2,128)(2,1)S(1)} %multiply_convert_fusion.7), channel_id=1, replica_groups=mesh['seq_0'=4,'seq_1'=2,'seq_2'=4,'seq_3'=2,'tp'=2] {'seq_0'}, dimensions={0}, use_global_device_ids=true | all-gather | bytes 240 | tf_op jit(solution)/shard_map/all_gather | solution.py:29
  104.7 15.2 %all-gather.10.cloned.1.call-done = bf16[4,24,64,128]{3,2,1,0:T(8,128)(2,1)} async-done(((bf16[1,24,64,128]{3,2,1,0:T(8,128)(2,1)}), bf16[4,24,64,128]{3,2,1,0:T(8,128)(2,1)}) %all-gather.10.cloned.1.call-update) | async-done | bytes 1572880 | tf_op jit(solution)/shard_map/all_gather | solution.py:29
  119.9 3.7 %fusion.35 = f32[24,64,128]{2,1,0:T(8,128)S(1)} fusion(bf16[4,24,64,128]{3,2,1,0:T(8,128)(2,1)} %all-gather.10.cloned.1.call-done, f32[24]{0:T(128)} %get-tuple-element.90, f32[24]{0:T(128)} %get-tuple-element.89, f32[24]{0:T(128)S(1)} %get-tuple-element.104, f32[24]{0:T(128)S(1)} %slice_convert_fusion.7, f32[24]{0:T(128)S(1)} %get-tuple-element.99, ...), kind=kLoop, calls=%fused_computation.57 | loop fusion | flops 9830400 | bytes 5506476 | tf_op jit(solution)/shard_map/mul | solution.py:335
  125.6 4.0 %multiply_reduce_fusion = (f32[2,256,24]{1,2,0:T(8,128)S(1)}, f32[2,256,24,64]{1,3,2,0:T(8,128)S(1)}) fusion(f32[2,24,64,256]{3,2,1,0:T(8,128)S(1)} %fusion.22, f32[2,256,24]{1,2,0:T(8,128)S(1)} %copy-done.11, f32[2,256,24,64]{1,3,2,0:T(8,128)S(1)} %copy-done.2, f32[24]{0:T(128)S(1)} %copy-done.16, f32[2,256,256]{2,1,0:T(8,128)S(1)} %copy-done.7, ...), kind=kOutput, calls=%fused_computation.36 | convolution fusion | flops 424660992 | bytes 10223712 | tf_op jit(solution)/shard_map/vmap(hts,shp->thp)/dot_general | solution.py:270
  129.6 2.5 copy.93
  134.3 5.4 %convolution_convert_fusion = bf16[512,3072]{1,0:T(8,128)(2,1)S(1)} fusion(bf16[512,1536]{0,1:T(8,128)(2,1)S(1)} %fusion.17, bf16[1536,3072]{1,0:T(8,128)(2,1)S(1)} %bitcast.210), kind=kOutput, calls=%fused_computation.22 | convolution fusion | flops 4833411072 | bytes 14155776 | tf_op jit(solution)/shard_map/dot_general | solution.py:347
  140.0 38.7 %all_to_all.16 = bf16[2,512,1536]{2,1,0:T(8,128)(2,1)S(1)} all-to-all(bf16[2,512,1536]{2,1,0:T(8,128)(2,1)S(1)} %bitcast.192), channel_id=1, replica_groups=mesh['seq_0'=4,'seq_1'=2,'seq_2'=4,'seq_3'=2,'tp'=2] {'tp'}, dimensions={0} | all-to-all | bytes 6291456 | tf_op jit(solution)/shard_map/all_to_all | solution.py:52
  181.2 3.2 %all-to-all-start.1 = ((f32[2,1,512]{2,1,0:T(1,128)}), f32[2,1,512]{2,1,0:T(1,128)S(1)}, u32[]{:S(2)}, u32[]{:S(2)}) async-start(f32[2,1,512]{2,1,0:T(1,128)} %broadcast_in_dim.45), calls=%async_computation.1 | async-start | bytes 8192 | tf_op jit(solution)/shard_map/all_to_all | solution.py:58
  184.5 3.7 %all-to-all-done.1 = f32[2,1,512]{2,1,0:T(1,128)S(1)} async-done(((f32[2,1,512]{2,1,0:T(1,128)}), f32[2,1,512]{2,1,0:T(1,128)S(1)}, u32[]{:S(2)}, u32[]{:S(2)}) %all-to-all-start.1) | async-done | bytes 4128 | tf_op jit(solution)/shard_map/all_to_all | solution.py:58
  189.7 36.9 %all_to_all.17 = bf16[2,512,1536]{1,2,0:T(8,128)(2,1)S(1)} all-to-all(bf16[2,512,1536]{1,2,0:T(8,128)(2,1)S(1)} %broadcast_in_dim.46), channel_id=1, replica_groups=mesh['seq_0'=4,'seq_1'=2,'seq_2'=4,'seq_3'=2,'tp'=2] {'tp'}, dimensions={0} | all-to-all | bytes 6291456 | tf_op jit(solution)/shard_map/all_to_all | solution.py:58
  226.6 5.2 %fusion.26 = bf16[512,768]{1,0:T(8,128)(2,1)S(1)} fusion(bf16[512,3072]{0,1:T(8,128)(2,1)S(1)} %bitcast.193, bf16[3,3072,768]{2,1,0:T(8,128)(2,1)} %bitcast.204), kind=kOutput, calls=%fused_computation.46 | convolution fusion | flops 2416312320 | bytes 8650752 | tf_op jit(solution)/shard_map/dot_general | solution.py:363
  231.8 2.7 fusion.27
  234.5 2.7 fusion.28
  238.8 65.1 %attn.1 = bf16[512,768]{1,0:T(8,128)(2,1)} custom-call(bf16[512,2304]{1,0:T(8,128)(2,1)} %pad_maximum_fusion.proj_ref), custom_call_target="tpu_custom_call" | custom-call | tf_op jit(solution)/shard_map/attn/pallas_call | solution.py:240
  (113 shorter events, 26.1 us)
Async XLA Ops:
  7.2 96.5 %copy-start = (bf16[512,128]{1,0:T(8,128)(2,1)S(1)}, bf16[512,128]{1,0:T(8,128)(2,1)}, u32[]{:S(2)}) copy-start(bf16[512,128]{1,0:T(8,128)(2,1)} %param.15) | copy-start | bytes 393220
  7.2 71.3 %all-gather.8.cloned.1.call-start = ((), (), s32[]{:S(2)}) async-start(), calls=%async_computation.3 | async-start | bytes 1966080 | tf_op jit(solution)/shard_map/all_gather | solution.py:29
  16.2 6.2 %copy-start.9 = (f32[512,24]{0,1:T(8,128)S(1)}, f32[512,24]{0,1:T(8,128)}, u32[]{:S(2)}) copy-start(f32[512,24]{0,1:T(8,128)} %param.16) | copy-start | bytes 147460
  16.2 6.2 %copy-start.8 = (bf16[512,128]{1,0:T(8,128)(2,1)S(1)}, bf16[512,128]{1,0:T(8,128)(2,1)}, u32[]{:S(2)}) copy-start(bf16[512,128]{1,0:T(8,128)(2,1)} %param.14) | copy-start | bytes 393220
  26.0 2.4 copy-start.17
  28.3 50.1 %copy-start.14 = (f32[2,24]{1,0:T(2,128)}, f32[2,24]{1,0:T(2,128)S(1)}, u32[]{:S(2)}) copy-start(f32[2,24]{1,0:T(2,128)S(1)} %get-tuple-element.42) | copy-start | bytes 580
  52.0 67.8 %all-gather.10.cloned.1.call-start = ((), (), s32[]{:S(2)}) async-start(), calls=%async_computation.4 | async-start | bytes 1966080 | tf_op jit(solution)/shard_map/all_gather | solution.py:29
  78.5 41.4 %copy-start.3 = (bf16[4,24,64,128]{3,2,1,0:T(8,128)(2,1)S(1)}, bf16[4,24,64,128]{3,2,1,0:T(8,128)(2,1)}, u32[]{:S(2)}) copy-start(bf16[4,24,64,128]{3,2,1,0:T(8,128)(2,1)} %all-gather.8.cloned.1.call-done) | copy-start | bytes 4718596
  104.7 19.0 %copy-start.15 = (f32[2,24]{1,0:T(2,128)S(1)}, f32[2,24]{1,0:T(2,128)}, u32[]{:S(2)}) copy-start(f32[2,24]{1,0:T(2,128)} %copy-done.14) | copy-start | bytes 580
  119.8 3.8 %copy-start.6 = (f32[2,24,64,128]{3,2,1,0:T(8,128)S(1)}, f32[2,24,64,128]{3,2,1,0:T(8,128)}, u32[]{:S(2)}) copy-start(f32[2,24,64,128]{3,2,1,0:T(8,128)} %get-tuple-element.45) | copy-start | bytes 4718596
  123.6 2.0 copy-start.7
  123.6 2.0 copy-start.10
  123.6 2.0 copy-start.11
  129.6 3.6 %slice-start.4 = ((s8[9437184]{0:T(1024)(128)(4,1)}), s8[1048576]{0:T(1024)(128)(4,1)S(1)}, s32[]{:S(2)}) async-start(s8[9437184]{0:T(1024)(128)(4,1)} %bitcast.209), calls=%async_computation.9 | async-start | bytes 2097152
  129.6 3.6 %slice-start.5 = ((s8[9437184]{0:T(1024)(128)(4,1)}), s8[4194304]{0:T(1024)(128)(4,1)S(1)}, s32[]{:S(2)}) async-start(s8[9437184]{0:T(1024)(128)(4,1)} %bitcast.209), calls=%async_computation.10 | async-start | bytes 8388608
  132.1 2.2 slice-start.6
  180.0 4.4 %copy-start.13 = (f32[3072]{0:T(1024)S(1)}, f32[3072]{0:T(1024)}, u32[]{:S(2)}) copy-start(f32[3072]{0:T(1024)} %param.22) | copy-start | bytes 36868
  180.6 7.7 %copy-start.4 = (bf16[512,1536]{1,0:T(8,128)(2,1)}, bf16[512,1536]{1,0:T(8,128)(2,1)S(1)}, u32[]{:S(2)}) copy-start(bf16[512,1536]{1,0:T(8,128)(2,1)S(1)} %get-tuple-element.185) | copy-start | bytes 4718596
  181.2 7.0 %all-to-all-start.1 = ((f32[2,1,512]{2,1,0:T(1,128)}), f32[2,1,512]{2,1,0:T(1,128)S(1)}, u32[]{:S(2)}, u32[]{:S(2)}) async-start(f32[2,1,512]{2,1,0:T(1,128)} %broadcast_in_dim.45), calls=%async_computation.1 | async-start | bytes 8192 | tf_op jit(solution)/shard_map/all_to_all | solution.py:58
  189.4 42.4 %slice-start = ((s8[14155776]{0:T(1024)(128)(4,1)}), s8[1572864]{0:T(1024)(128)(4,1)S(1)}, s32[]{:S(2)}) async-start(s8[14155776]{0:T(1024)(128)(4,1)} %bitcast.205), calls=%async_computation.5 | async-start | bytes 3145728
  189.7 42.1 %slice-start.1 = ((s8[14155776]{0:T(1024)(128)(4,1)}), s8[4194304]{0:T(1024)(128)(4,1)S(1)}, s32[]{:S(2)}) async-start(s8[14155776]{0:T(1024)(128)(4,1)} %bitcast.205), calls=%async_computation.6 | async-start | bytes 8388608
  226.6 5.2 %slice-start.2 = ((s8[14155776]{0:T(1024)(128)(4,1)}), s8[4194304]{0:T(1024)(128)(4,1)S(1)}, s32[]{:S(2)}) async-start(s8[14155776]{0:T(1024)(128)(4,1)} %bitcast.205), calls=%async_computation.7 | async-start | bytes 8388608
  226.6 5.2 %slice-start.3 = ((s8[14155776]{0:T(1024)(128)(4,1)}), s8[4194304]{0:T(1024)(128)(4,1)S(1)}, s32[]{:S(2)}) async-start(s8[14155776]{0:T(1024)(128)(4,1)} %bitcast.205), calls=%async_computation.8 | async-start | bytes 8388608
  237.2 68.8 %copy-start.1 = (bf16[512,128]{1,0:T(8,128)(2,1)S(1)}, bf16[512,128]{1,0:T(8,128)(2,1)}, u32[]{:S(2)}) copy-start(bf16[512,128]{1,0:T(8,128)(2,1)} %param.15) | copy-start | bytes 393220
  (4 other events, 6.0 us)
Sparse Core Ops, SparseCore 0:
  52.2 26.2 all-gather.7
  94.5 25.3 all-gather.9

commit v2 on v1

--- a/solution.py
+++ b/solution.py
@@ -14,33 +14,6 @@
 EPSILON = 1e-05
 
 
-def filled_with(x, identity):
-    return jax.tree.map(
-        lambda a, e: jnp.broadcast_to(jnp.asarray(e, a.dtype), a.shape), x, identity
-    )
-
-
-def carried_in(x, axes, combine, identity):
-    before = start = filled_with(x, identity)
-    running = x
-    for axis in reversed(axes):
-        size, position = (lax.axis_size(axis), lax.axis_index(axis))
-        pieces = jax.tree.map(
-            lambda part, kind: lax.all_gather(part.astype(kind), axis),
-            running,
-            jax.tree.map(lambda a: jnp.bfloat16 if a.dtype == jnp.float32 else a.dtype, x),
-        )
-        inside, running = (start, start)
-        for k in range(size):
-            passed = k < position
-            running = combine(
-                running, jax.tree.map(lambda part, own: part[k].astype(own.dtype), pieces, x)
-            )
-            inside = jax.tree.map(lambda new, old: jnp.where(passed, new, old), running, inside)
-        before = combine(inside, before)
-    return before
-
-
 def split_up(x, dim, size):
     lengths = x.shape
     pieces = x.reshape(*lengths[:dim], size, lengths[dim] // size, *lengths[dim + 1 :])
@@ -71,12 +44,6 @@
 
 def gathered_copies(x, axis, dim):
     return joined_along(from_everyone(x, axis), dim)
-
-
-def shifted(x, axis, by):
-    size = lax.axis_size(axis)
-    pairs = [(i, i + by) for i in range(size) if 0 <= i + by < size]
-    return lax.ppermute(x, axis, pairs)
 
 
 MESH = pl.DeviceIdType.MESH
@@ -252,45 +219,267 @@
             collective_id=3, has_side_effects=True, vmem_limit_bytes=56 * 2**20),
     )(proj)
 
-
-def span_terms(inputs, write_rows, read_rows, step_rows, decays, skip_gain):
-    length, head_count = step_rows.shape
-    head_dim = inputs.shape[1] // head_count
-    cumulative = jnp.cumsum(decays, axis=0)
-    totals = cumulative[-1]
-    values = inputs.astype(jnp.float32).reshape(length, head_count, head_dim)
-    scaled = (step_rows[:, :, None] * values).astype(jnp.bfloat16)
-    intersection = jnp.dot(read_rows, write_rows.T, preferred_element_type=jnp.float32)
-    sequence_place = jnp.arange(length)
-    causal = sequence_place[:, None] >= sequence_place[None, :]
-    log_gaps = cumulative.T[:, :, None] - cumulative.T[:, None, :]
-    mixing = (
-        jnp.where(causal, jnp.exp(jnp.where(causal, log_gaps, 0.0)), 0.0) * intersection
-    ).astype(jnp.bfloat16)
-    inner_part = jnp.einsum("hts,shp->thp", mixing, scaled, preferred_element_type=jnp.float32)
-    local_part = inner_part + skip_gain[None, :, None] * values
-    written = jnp.exp(totals[None, :] - cumulative)[:, :, None] * scaled.astype(jnp.float32)
-    state_term = jnp.einsum(
-        "shp,sn->hpn", written, write_rows.astype(jnp.float32), precision=lax.Precision.HIGHEST
-    )
-    return (local_part, state_term, totals, cumulative)
-
-
-def join_states(earlier_pair, later_pair):
-    return (
-        earlier_pair[0] * later_pair[0],
-        later_pair[0][:, None, None] * earlier_pair[1] + later_pair[1],
-    )
-
-
-def fold_spans(running, span_piece):
-    state_term, totals = span_piece
-    decay_run, state_run = running
-    factor = jnp.exp(totals)
-    return (
-        (decay_run * factor, factor[:, None, None] * state_run + state_term),
-        (decay_run, state_run),
-    )
+def parts_of(v, count):
+    out = []
+    for _ in range(count):
+        piece = v.astype(BF16)
+        out.append(piece)
+        v = v - piece.astype(F32)
+    return out
+
+
+def one_hot(shape, per_lane, period=None):
+    r = lax.broadcasted_iota(jnp.int32, shape, 0)
+    c = lax.broadcasted_iota(jnp.int32, shape, 1)
+    if period is not None:
+        r = lax.rem(r, period)
+    return jnp.where(r == c // per_lane, 1.0, 0.0).astype(BF16)
+
+
+def mixer_kernel(x_ref, b_ref, c_ref, step_ref, ld_ref, skip_ref, hg_ref, n_ref,
+                 u, ybuf, eexp, gexp, gt, s0, stage, rs, pref, dpre, rowst, rr, back, cin,
+                 tst, tr, rtst, rtr,
+                 a_send, a_recv, at_send, at_recv, r_send, r_recv, rt_send, rt_recv,
+                 c_send, c_recv):
+    z = lax.axis_index("seq_0")
+    yh = lax.axis_index("seq_1")
+    xx = lax.axis_index("seq_2")
+    cc = lax.axis_index("seq_3")
+    g = xx * 2 + cc
+    row = z * 2 + yh
+    nh, blk, wid = 24, 256, 1536
+
+    def at_group(j):
+        return {"seq_2": j // 2, "seq_3": lax.rem(j, 2)}
+
+    def at_row(r):
+        return {"seq_0": r // 2, "seq_1": lax.rem(r, 2)}
+
+    barrier = pltpu.get_barrier_semaphore()
+    for d in range(1, 8):
+        pl.semaphore_signal(barrier, inc=1, device_id=at_group(lax.rem(g + d, 8)), device_id_type=MESH)
+        pl.semaphore_signal(barrier, inc=1, device_id=at_row(lax.rem(row + d, 8)), device_id_type=MESH)
+
+    def dot(a, b):
+        return jnp.dot(a, b, preferred_element_type=F32)
+
+    si = lax.broadcasted_iota(jnp.int32, (blk, blk), 0)
+    ti = lax.broadcasted_iota(jnp.int32, (blk, blk), 1)
+    upto = jnp.where(si <= ti, 1.0, 0.0).astype(BF16)
+    wt = []
+    for c in range(2):
+        ld = ld_ref[:, c * blk:(c + 1) * blk]
+        cat = jnp.concatenate(parts_of(ld, 3), axis=0)
+        r = dot(cat, upto)
+        gtc = (r[0:nh] + r[nh:2 * nh] + r[2 * nh:3 * nh]) * LOG2E
+        gt[:, c * blk:(c + 1) * blk] = gtc
+        wt.append(jnp.exp2(gtc[:, blk - 1:blk] - gtc))
+    gtv = gt[...]
+    g_col = gtv.T
+    total = g_col[blk - 1:blk] + g_col[2 * blk - 1:2 * blk]
+    tst[...] = jnp.zeros((8, 128), F32)
+    tst[0:1, 0:nh] = total
+
+    e3 = one_hot((3 * nh, wid), 64, nh)
+
+    def expand(v, count=3):
+        k = count * nh
+        return dot(jnp.concatenate(parts_of(v, count), axis=1), e3[0:k] if count < 3 else e3)
+
+    step_col = step_ref[...].T
+    w_col = jnp.concatenate(wt, axis=1).T
+    e_col = jnp.exp2(g_col)
+    eexp[...] = expand(e_col)
+    one3 = one_hot((3 * nh, nh * 128), 128, nh)
+    gexp[...] = dot(jnp.concatenate(parts_of(g_col, 3), axis=1), one3)
+    state = None
+    for c in range(2):
+        rows = slice(c * blk, (c + 1) * blk)
+        uc = (expand(step_col[rows]) * x_ref[rows].astype(F32)).astype(BF16)
+        u[rows] = uc
+        wu = (expand(w_col[rows]) * uc.astype(F32)).astype(BF16)
+        term = dot(b_ref[rows].T, wu)
+        if c == 0:
+            s0[...] = term
+        else:
+            state = eexp[2 * blk - 1:2 * blk] * s0[...] + term
+    stage[...] = state.astype(BF16)
+    pl.semaphore_wait(barrier, 14)
+
+    def slice_of(j):
+        return pl.ds(pl.multiple_of(j * 16, 16), 16)
+
+    def a_copy(d):
+        j = lax.rem(g + d, 8)
+        return pltpu.make_async_remote_copy(
+            src_ref=stage.at[slice_of(j)], dst_ref=rs.at[g],
+            send_sem=a_send.at[d], recv_sem=a_recv.at[g],
+            device_id=at_group(j), device_id_type=MESH)
+
+    def at_copy(d):
+        j = lax.rem(g + d, 8)
+        return pltpu.make_async_remote_copy(
+            src_ref=tst, dst_ref=tr.at[g],
+            send_sem=at_send.at[d], recv_sem=at_recv.at[g],
+            device_id=at_group(j), device_id_type=MESH)
+
+    def r_copy(d):
+        return pltpu.make_async_remote_copy(
+            src_ref=rowst, dst_ref=rr.at[row],
+            send_sem=r_send.at[d], recv_sem=r_recv.at[row],
+            device_id=at_row(lax.rem(row + d, 8)), device_id_type=MESH)
+
+    def rt_copy(d):
+        return pltpu.make_async_remote_copy(
+            src_ref=rtst, dst_ref=rtr.at[row],
+            send_sem=rt_send.at[d], recv_sem=rt_recv.at[row],
+            device_id=at_row(lax.rem(row + d, 8)), device_id_type=MESH)
+
+    def c_copy(j):
+        return pltpu.make_async_remote_copy(
+            src_ref=back.at[j], dst_ref=cin.at[slice_of(g)],
+            send_sem=c_send.at[j], recv_sem=c_recv.at[g],
+            device_id=at_group(j), device_id_type=MESH)
+
+    def landed(ref, sem):
+        pltpu.make_async_copy(ref, ref, sem).wait()
+
+    for d in range(1, 8):
+        at_copy(d).start()
+    for d in (4, 5, 3, 2, 6, 1, 7):
+        a_copy(d).start()
+    rs[g] = stage[slice_of(g), :]
+    tr[g] = tst[...]
+
+    causal = si >= ti
+
+    def local_pairs(c, lo, hi):
+        rows = slice(c * blk, (c + 1) * blk)
+        cb = lax.dot_general(c_ref[rows], b_ref[rows], (((1,), (1,)), ((), ())),
+                             preferred_element_type=F32)
+        cb = jnp.where(causal, cb, 0.0)
+        lane = lax.broadcasted_iota(jnp.int32, (blk, 128), 1)
+
+        def pair(p, _):
+            off = pl.multiple_of(p * 128, 128)
+            up = u[rows, pl.ds(off, 128)]
+            ys = []
+            for k in range(2):
+                h = p * 2 + k
+                gc = gexp[rows, pl.ds(pl.multiple_of(h * 128, 128), 128)]
+                gr = gt[pl.ds(h, 1), rows]
+                gap = jnp.concatenate([gc, gc], axis=1) - gr
+                m = (jnp.exp2(jnp.minimum(gap, 0.0)) * cb).astype(BF16)
+                ys.append(dot(m, up))
+            ybuf[rows, pl.ds(off, 128)] = jnp.where(lane < 64, ys[0], ys[1])
+            return 0
+
+        lax.fori_loop(lo, hi, pair, 0)
+
+    local_pairs(0, 0, 12)
+
+    for j in range(8):
+        @pl.when(j != g)
+        def _(j=j):
+            landed(tr.at[j], at_recv.at[j])
+            landed(rs.at[j], a_recv.at[j])
+    e128 = one_hot((128, wid), 64)
+
+    def table(ref):
+        t = jnp.concatenate([ref[j, 0:1, :] for j in range(8)], axis=0)
+        return t
+
+    def spread(t):
+        p = parts_of(t, 3)
+        return dot(p[0], e128) + dot(p[1], e128) + dot(p[2], e128)
+
+    tt = table(tr)
+    dec = spread(jnp.exp2(tt))
+    run = jnp.zeros((16, wid), F32)
+    dr = jnp.ones((1, wid), F32)
+    for j in range(8):
+        pref[j] = run
+        dpre[j:j + 1] = dr
+        run = run * dec[j:j + 1] + rs[j].astype(F32)
+        dr = dr * dec[j:j + 1]
+    rowst[...] = run.astype(BF16)
+    rtst[...] = jnp.broadcast_to(jnp.sum(tt, axis=0, keepdims=True), (8, 128))
+    for d in range(1, 8):
+        @pl.when(row + d < 8)
+        def _(d=d):
+            rt_copy(d).start()
+            r_copy(d).start()
+
+    local_pairs(1, 0, 8)
+
+    for r in range(7):
+        @pl.when(r < row)
+        def _(r=r):
+            landed(rtr.at[r], rt_recv.at[r])
+            landed(rr.at[r], r_recv.at[r])
+    rmask = lax.broadcasted_iota(jnp.int32, (8, 128), 0) < row
+    rdec = spread(jnp.where(rmask, jnp.exp2(table(rtr)), 0.0))
+    rc = jnp.zeros((16, wid), F32)
+    for r in range(7):
+        rc = jnp.where(r < row, rc * rdec[r:r + 1] + rr[r].astype(F32), rc)
+    for j in range(8):
+        back[j] = (pref[j] + dpre[j:j + 1] * rc).astype(BF16)
+    for d in (4, 5, 3, 2, 6, 1, 7):
+        c_copy(lax.rem(g + d, 8)).start()
+    cin[slice_of(g), :] = back[g]
+
+    local_pairs(1, 8, 12)
+
+    skip = expand(jnp.broadcast_to(skip_ref[...], (8, nh)))[0:1]
+    et = jnp.where(lax.broadcasted_iota(jnp.int32, (wid, nh), 0) // 64
+                   == lax.broadcasted_iota(jnp.int32, (wid, nh), 1), 1.0, 0.0).astype(BF16)
+    for j in range(8):
+        @pl.when(j != g)
+        def _(j=j):
+            landed(cin.at[pl.ds(j * 16, 16)], c_recv.at[j])
+    entering = cin[...].astype(F32)
+    for c in range(2):
+        rows = slice(c * blk, (c + 1) * blk)
+        if c == 1:
+            entering = eexp[blk - 1:blk] * entering + s0[...]
+        y = ybuf[rows] + eexp[rows] * dot(c_ref[rows], entering.astype(BF16))
+        y = y + skip * x_ref[rows].astype(F32)
+        sq = parts_of(y * y, 2)
+        ssum = dot(sq[0], et) + dot(sq[1], et)
+        inv = lax.rsqrt(ssum * (1.0 / 64.0) + EPSILON)
+        n_ref[rows] = (y * expand(inv) * hg_ref[...]).astype(BF16)
+
+    for d in range(1, 8):
+        at_copy(d).wait_send()
+        a_copy(d).wait_send()
+        c_copy(lax.rem(g + d, 8)).wait_send()
+
+        @pl.when(row + d < 8)
+        def _(d=d):
+            rt_copy(d).wait_send()
+            r_copy(d).wait_send()
+
+
+def mixer(x, b, c, step, ld, skip, hg):
+    V = pltpu.VMEM
+    D = pltpu.SemaphoreType.DMA
+    wid = 1536
+    return pl.pallas_call(
+        mixer_kernel,
+        name="mixer",
+        out_shape=jax.ShapeDtypeStruct((512, wid), BF16),
+        in_specs=[pl.BlockSpec(memory_space=V)] * 7,
+        out_specs=pl.BlockSpec(memory_space=V),
+        scratch_shapes=[
+            V((512, wid), BF16), V((512, wid), F32), V((512, wid), F32), V((512, 3072), F32),
+            V((24, 512), F32), V((128, wid), F32), V((128, wid), BF16), V((8, 16, wid), BF16),
+            V((8, 16, wid), F32), V((8, wid), F32), V((16, wid), BF16), V((8, 16, wid), BF16),
+            V((8, 16, wid), BF16), V((128, wid), BF16),
+            V((8, 128), F32), V((8, 8, 128), F32), V((8, 128), F32), V((8, 8, 128), F32),
+        ] + [D((8,))] * 10,
+        compiler_params=pltpu.CompilerParams(
+            collective_id=1, has_side_effects=True, vmem_limit_bytes=60 * 2**20),
+    )(x, b, c, step.T, ld.T, skip.reshape(1, 24), hg.reshape(1, wid))
 
 
 def on_device(
@@ -310,40 +499,7 @@
     head_count = step_size.shape[1]
     channels = mixer_input.shape[1]
     head_dim = channels // head_count
-    span_len = min(tokens_dev, 256)
-    span_count = tokens_dev // span_len
-
-    def blocked(tensor):
-        return tensor.reshape((span_count, span_len) + tensor.shape[1:])
-
-    local_part, state_terms, totals, cumulative = jax.vmap(
-        span_terms, in_axes=(0, 0, 0, 0, 0, None)
-    )(
-        blocked(mixer_input),
-        blocked(state_write),
-        blocked(state_read),
-        blocked(step_size),
-        blocked(log_decay),
-        skip_gain,
-    )
-    identity_pair = (
-        jnp.ones((head_count,), jnp.float32),
-        jnp.zeros((head_count, head_dim, state_write.shape[1]), jnp.float32),
-    )
-    device_pair, before = lax.scan(fold_spans, identity_pair, (state_terms, totals))
-    carry_in = carried_in(device_pair, SEQ, join_states, identity_pair)
-    entering = before[0][:, :, None, None] * carry_in[1][None] + before[1]
-    from_before = jnp.exp(cumulative)[..., None] * jnp.einsum(
-        "ctn,chpn->cthp",
-        blocked(state_read).astype(jnp.float32),
-        entering,
-        precision=lax.Precision.HIGHEST,
-    )
-    head_outputs = (local_part + from_before).reshape(tokens_dev, head_count, head_dim)
-    inverse_rms = lax.rsqrt(jnp.mean(head_outputs * head_outputs, axis=2, keepdims=True) + EPSILON)
-    normed = ((head_outputs * inverse_rms).reshape(tokens_dev, channels) * head_gain).astype(
-        jnp.bfloat16
-    )
+    normed = mixer(mixer_input, state_write, state_read, step_size, log_decay, skip_gain, head_gain)
     partial_value = jnp.dot(normed, mixer_out, preferred_element_type=jnp.float32)
     model_width = partial_value.shape[1]
     half_width = residual.shape[1]

time: 315 us -> 208 us (0.66)
  waiting for transfers between devices: 45.2 us -> 3.68 us
  blocking collectives: 117 us -> 76.4 us
  Pallas kernels: 65.1 us -> 95.3 us
  local copies, waits for them, and re-layouts: 23 us -> 6.1 us
  other arithmetic: 18.2 us -> 3.11 us
  between operations: 15.2 us -> 0.81 us
  matrix products: 26 us -> 18.7 us
    all_gather x2 -> x0, waiting for transfers between devices: 41.5 us -> none  [carried_in(): lax.all_gather(part.astype(kind), axis)]
    all_gather x5 -> x0, blocking collectives: 38.8 us -> none  [carried_in(): lax.all_gather(part.astype(kind), axis)]
    pallas_call x0 -> x1, Pallas kernels: none -> 30.9 us  [mixer(): pl.pallas_call(mixer_kernel, name='mixer', out_shape=jax.ShapeDtypeStruct...]
    convert_element_type x2 -> x0, local copies, waits for them, and re-layouts: 11.4 us -> none  [span_terms(): values = inputs.astype(jnp.float32).reshape(length, head_count, head_dim)]
    dot_general x4 -> x0, matrix products: 10.1 us -> none  [the longest x1 4.03 us: span_terms(): jnp.einsum('hts,shp->thp', mixing, scaled, preferred_element_type=jnp.flo...]
    convert_element_type x11 -> x0, other arithmetic: 5.2 us -> none  [the longest x6 4.11 us: carried_in(): part.astype(kind)]
    mul x5 -> x0, other arithmetic: 4.93 us -> none  [the longest x1 3.72 us: on_device(): entering = before[0][:, :, None, None] * carry_in[1][None] + before[1]]
  transfers between devices with their start and end apart: 3 -> 1, of which waited for: 3 -> 1; matrix products, arithmetic and copies ran while one was open for 1% -> 0% of each run, Pallas kernels for 0% -> 0%
where the time goes in v2:
time: 208 us; the launch traced here: 207 us
  Pallas kernels  95.3 us (46%)
  blocking collectives  76.4 us (37%)
  matrix products  18.7 us (9%)
  local copies, waits for them, and re-layouts  6.1 us (3%)
  waiting for transfers between devices  3.68 us (2%)
  starting transfers between devices  3.22 us (2%)
  other arithmetic  3.11 us (1%)
    pallas_call x1, Pallas kernels, attention(): pl.pallas_call(attn_kernel, name='attn', out_shape=jax.ShapeDtypeStruct((...  64.4 us
    all_to_all x1, blocking collectives, sum_at_owner(): lax.all_to_all(pieces, axis, split_axis=0, concat_axis=0, tiled=True)  39.1 us
    all_to_all x1, blocking collectives, from_everyone(): lax.all_to_all(jnp.broadcast_to(x[None], (size, *x.shape)), axis, 0, 0, t...  37.4 us
    pallas_call x1, Pallas kernels, mixer(): pl.pallas_call(mixer_kernel, name='mixer', out_shape=jax.ShapeDtypeStruct...  30.9 us
    dot_general x3, matrix products, on_device(): jnp.dot(normed_stream, weight[i], preferred_element_type=jnp.float32)  10.6 us
    dot_general x1, matrix products, on_device(): jnp.dot(normed, mixer_out, preferred_element_type=jnp.float32)  8.09 us
  transfers between devices with their start and end apart: 1, of which 1 were waited for; matrix products, arithmetic and copies ran while one was open for 0% of the time, Pallas kernels for 0%

profile of v2, /device:TPU:32, one launch (start us, length us, event | category | flops | bytes accessed | tf_op | source)
XLA Modules:
  0.0 207.4 jit_solution(17163542548040903298)
XLA Ops:
  0.6 1.3 reshape.30.hg_ref
  1.9 30.9 %mixer.1 = bf16[512,1536]{1,0:T(8,128)(2,1)} custom-call(bf16[512,1536]{1,0:T(8,128)(2,1)} %x_ref.1, bf16[512,128]{1,0:T(8,128)(2,1)} %b_ref.1, bf16[512,128]{1,0:T(8,128)(2,1)} %c_ref.1, f32[24,512]{1,0:T(8,128)} %bitcast.39, f32[24,512]{1,0:T(8,128)} %bitcast.40, f32[1,24]{1,0:T(1,128)} %bitcast.41, f32[1,1536]{1,0:T(1,128)} %reshape.30.hg_ref), custom_call_target="tpu_custom_call" | custom-call | tf_op jit(solution)/shard_map/mixer/pallas_call | solution.py:467
  32.8 8.1 %convolution_convert_fusion = bf16[512,3072]{1,0:T(8,128)(2,1)S(1)} fusion(bf16[512,1536]{1,0:T(8,128)(2,1)} %mixer.1, bf16[1536,3072]{1,0:T(8,128)(2,1)} %param.18), kind=kOutput, calls=%fused_computation.7 | convolution fusion | flops 4833411072 | bytes 14155776 | tf_op jit(solution)/shard_map/dot_general | solution.py:503
  40.9 0.2 copy.24
  41.2 39.1 %all_to_all.16 = bf16[2,512,1536]{2,1,0:T(8,128)(2,1)S(1)} all-to-all(bf16[2,512,1536]{2,1,0:T(8,128)(2,1)S(1)} %bitcast.34), channel_id=1, replica_groups=mesh['seq_0'=4,'seq_1'=2,'seq_2'=4,'seq_3'=2,'tp'=2] {'tp'}, dimensions={0} | all-to-all | bytes 6291456 | tf_op jit(solution)/shard_map/all_to_all | solution.py:25
  80.3 0.6 convert_reduce_fusion
  80.8 0.8 copy-done.1
  81.7 0.5 fusion.3
  82.2 0.6 broadcast_in_dim.4
  82.9 3.2 %all-to-all-start.1 = ((f32[2,1,512]{2,1,0:T(1,128)}), f32[2,1,512]{2,1,0:T(1,128)S(1)}, u32[]{:S(2)}, u32[]{:S(2)}) async-start(f32[2,1,512]{2,1,0:T(1,128)} %broadcast_in_dim.4), calls=%async_computation.1 | async-start | bytes 8192 | tf_op jit(solution)/shard_map/all_to_all | solution.py:31
  86.1 0.1 dynamic_slice.3
  86.2 3.7 %all-to-all-done.1 = f32[2,1,512]{2,1,0:T(1,128)S(1)} async-done(((f32[2,1,512]{2,1,0:T(1,128)}), f32[2,1,512]{2,1,0:T(1,128)S(1)}, u32[]{:S(2)}, u32[]{:S(2)}) %all-to-all-start.1) | async-done | bytes 4128 | tf_op jit(solution)/shard_map/all_to_all | solution.py:31
  89.9 0.4 fusion.5
  90.3 0.7 copy.20
  91.1 0.0 slice-start
  91.1 0.2 broadcast_in_dim.5
  91.3 0.0 slice-start.1
  91.3 37.4 %all_to_all.17 = bf16[2,512,1536]{1,2,0:T(8,128)(2,1)S(1)} all-to-all(bf16[2,512,1536]{1,2,0:T(8,128)(2,1)S(1)} %broadcast_in_dim.5), channel_id=1, replica_groups=mesh['seq_0'=4,'seq_1'=2,'seq_2'=4,'seq_3'=2,'tp'=2] {'tp'}, dimensions={0} | all-to-all | bytes 6291456 | tf_op jit(solution)/shard_map/all_to_all | solution.py:31
  128.7 5.2 %fusion.8 = bf16[512,768]{1,0:T(8,128)(2,1)S(1)} fusion(bf16[512,3072]{0,1:T(8,128)(2,1)S(1)} %bitcast.35, bf16[3,3072,768]{2,1,0:T(8,128)(2,1)} %bitcast.42), kind=kOutput, calls=%fused_computation.18 | convolution fusion | flops 2416312320 | bytes 8650752 | tf_op jit(solution)/shard_map/dot_general | solution.py:519
  133.9 2.7 %fusion.7 = bf16[512,768]{1,0:T(8,128)(2,1)S(1)} fusion(bf16[512,3072]{0,1:T(8,128)(2,1)S(1)} %bitcast.36, bf16[3,3072,768]{2,1,0:T(8,128)(2,1)S(1)} %bitcast.45), kind=kOutput, calls=%fused_computation.17 | convolution fusion | flops 2416312320 | bytes 8650752 | tf_op jit(solution)/shard_map/dot_general | solution.py:519
  136.6 2.7 %fusion.6 = bf16[512,768]{1,0:T(8,128)(2,1)S(1)} fusion(bf16[512,3072]{0,1:T(8,128)(2,1)S(1)} %bitcast.37, bf16[3,3072,768]{2,1,0:T(8,128)(2,1)S(1)} %bitcast.46), kind=kOutput, calls=%fused_computation.16 | convolution fusion | flops 2416312320 | bytes 8650752 | tf_op jit(solution)/shard_map/dot_general | solution.py:519
  139.3 1.6 pad_maximum_fusion.proj_ref
  140.9 64.4 %attn.1 = bf16[512,768]{1,0:T(8,128)(2,1)} custom-call(bf16[512,2304]{1,0:T(8,128)(2,1)} %pad_maximum_fusion.proj_ref), custom_call_target="tpu_custom_call" | custom-call | tf_op jit(solution)/shard_map/attn/pallas_call | solution.py:207
  205.3 2.1 copy.26
  (14 shorter events, 0.1 us)
Async XLA Ops:
  80.3 1.4 copy-start.1
  81.7 4.4 %copy-start.2 = (f32[3072]{0:T(1024)S(1)}, f32[3072]{0:T(1024)}, u32[]{:S(2)}) copy-start(f32[3072]{0:T(1024)} %param.20) | copy-start | bytes 36868
  82.2 7.7 %copy-start = (bf16[512,1536]{1,0:T(8,128)(2,1)}, bf16[512,1536]{1,0:T(8,128)(2,1)S(1)}, u32[]{:S(2)}) copy-start(bf16[512,1536]{1,0:T(8,128)(2,1)S(1)} %get-tuple-element.6) | copy-start | bytes 4718596
  82.9 7.0 %all-to-all-start.1 = ((f32[2,1,512]{2,1,0:T(1,128)}), f32[2,1,512]{2,1,0:T(1,128)S(1)}, u32[]{:S(2)}, u32[]{:S(2)}) async-start(f32[2,1,512]{2,1,0:T(1,128)} %broadcast_in_dim.4), calls=%async_computation.1 | async-start | bytes 8192 | tf_op jit(solution)/shard_map/all_to_all | solution.py:31
  91.1 42.8 %slice-start = ((s8[14155776]{0:T(1024)(128)(4,1)}), s8[1572864]{0:T(1024)(128)(4,1)S(1)}, s32[]{:S(2)}) async-start(s8[14155776]{0:T(1024)(128)(4,1)} %bitcast.43), calls=%async_computation.3 | async-start | bytes 3145728
  91.3 42.6 %slice-start.1 = ((s8[14155776]{0:T(1024)(128)(4,1)}), s8[4194304]{0:T(1024)(128)(4,1)S(1)}, s32[]{:S(2)}) async-start(s8[14155776]{0:T(1024)(128)(4,1)} %bitcast.43), calls=%async_computation.4 | async-start | bytes 8388608
  128.7 5.2 %slice-start.2 = ((s8[14155776]{0:T(1024)(128)(4,1)}), s8[4194304]{0:T(1024)(128)(4,1)S(1)}, s32[]{:S(2)}) async-start(s8[14155776]{0:T(1024)(128)(4,1)} %bitcast.43), calls=%async_computation.5 | async-start | bytes 8388608
  128.7 5.2 %slice-start.3 = ((s8[14155776]{0:T(1024)(128)(4,1)}), s8[4194304]{0:T(1024)(128)(4,1)S(1)}, s32[]{:S(2)}) async-start(s8[14155776]{0:T(1024)(128)(4,1)} %bitcast.43), calls=%async_computation.6 | async-start | bytes 8388608

commit v3 on v2

--- a/solution.py
+++ b/solution.py
@@ -6,44 +6,10 @@
 from jax.experimental.pallas import tpu as pltpu
 from jax.sharding import PartitionSpec as P
 
-AHD = 96
-WINDOW = 2048
 SEQ = ("seq_0", "seq_1", "seq_2", "seq_3")
 
 
 EPSILON = 1e-05
-
-
-def split_up(x, dim, size):
-    lengths = x.shape
-    pieces = x.reshape(*lengths[:dim], size, lengths[dim] // size, *lengths[dim + 1 :])
-    return jnp.moveaxis(pieces, dim, 0)
-
-
-def sum_at_owner(x, axis, dim):
-    pieces = split_up(x, dim, lax.axis_size(axis))
-    arrived = lax.all_to_all(pieces, axis, split_axis=0, concat_axis=0, tiled=True)
-    return arrived.astype(jnp.float32).sum(axis=0)
-
-
-def from_everyone(x, axis):
-    size = lax.axis_size(axis)
-    return lax.all_to_all(jnp.broadcast_to(x[None], (size, *x.shape)), axis, 0, 0, tiled=True)
-
-
-def over_copies(x, axis):
-    everything = from_everyone(x, axis)
-    return jnp.sum(everything, axis=0)
-
-
-def joined_along(pieces, dim):
-    pieces = jnp.moveaxis(pieces, 0, dim)
-    lengths = pieces.shape
-    return pieces.reshape(*lengths[:dim], lengths[dim] * lengths[dim + 1], *lengths[dim + 2 :])
-
-
-def gathered_copies(x, axis, dim):
-    return joined_along(from_everyone(x, axis), dim)
 
 
 MESH = pl.DeviceIdType.MESH
@@ -52,172 +18,6 @@
 NEG = -1e30
 LOG2E = 1.4426950408889634
 
-
-def attn_kernel(proj_ref, out_ref, own, buf, knat, osend, oland, send_sem, recv_sem,
-                hsend_sem, hrecv_sem, osend_sem, orecv_sem):
-    z = lax.axis_index("seq_0")
-    yh = lax.axis_index("seq_1")
-    xx = lax.axis_index("seq_2")
-    cc = lax.axis_index("seq_3")
-    g = xx * 2 + cc
-    row = z * 2 + yh
-    nrow = lax.rem(row + 1, 8)
-    prow = lax.rem(row + 7, 8)
-    hd = 96
-    tok = 512
-
-    def at_group(j):
-        return {"seq_2": j // 2, "seq_3": lax.rem(j, 2)}
-
-    def at_row(r):
-        return {"seq_0": r // 2, "seq_1": lax.rem(r, 2)}
-
-    barrier = pltpu.get_barrier_semaphore()
-    for d in range(1, 8):
-        pl.semaphore_signal(barrier, inc=1, device_id=at_group(lax.rem(g + d, 8)), device_id_type=MESH)
-    pl.semaphore_signal(barrier, inc=1, device_id=at_row(nrow), device_id_type=MESH)
-    pl.semaphore_signal(barrier, inc=1, device_id=at_row(prow), device_id_type=MESH)
-    for i in range(3):
-        own[i] = proj_ref[:, i * 768:(i + 1) * 768].T
-    pl.semaphore_wait(barrier, 9)
-
-    def head(j):
-        return pl.ds(pl.multiple_of(j * hd, 32), hd)
-
-    def block_copy(d):
-        j = lax.rem(g + d, 8)
-        return pltpu.make_async_remote_copy(
-            src_ref=own.at[:, head(j), :],
-            dst_ref=buf.at[4 + g],
-            send_sem=send_sem.at[d],
-            recv_sem=recv_sem.at[g],
-            device_id=at_group(j), device_id_type=MESH)
-
-    def arrival(b):
-        return pltpu.make_async_copy(buf.at[4 + b], buf.at[4 + b], recv_sem.at[b])
-
-    def halo_copy(i):
-        return pltpu.make_async_remote_copy(
-            src_ref=buf.at[8 + i, pl.ds(1, 2)],
-            dst_ref=buf.at[i, pl.ds(1, 2)],
-            send_sem=hsend_sem.at[i],
-            recv_sem=hrecv_sem.at[i],
-            device_id=at_row(nrow), device_id_type=MESH)
-
-    for d in (4, 5, 3, 2, 6, 1, 7):
-        block_copy(d).start()
-    buf[4 + g] = own[:, head(g), :]
-
-    def arrived(b):
-        @pl.when(b != g)
-        def _():
-            arrival(b).wait()
-        knat[4 + b] = buf[4 + b, 1].T
-
-    for b in range(4, 8):
-        arrived(b)
-
-        @pl.when(row < 7)
-        def _(i=b - 4):
-            halo_copy(i).start()
-    for b in range(4):
-        arrived(b)
-
-    scale = (hd ** -0.5) * LOG2E
-    spos = lax.broadcasted_iota(jnp.int32, (tok, tok), 0)
-    tpos = lax.broadcasted_iota(jnp.int32, (tok, tok), 1)
-    causal = spos <= tpos
-
-    def one_block(step, _):
-        b = jnp.where(step < 4, 4 + step, 7 - step)
-
-        @pl.when(jnp.logical_and(step >= 4, row > 0))
-        def _():
-            halo_copy(b).wait_recv()
-            knat[b] = buf[b, 1].T
-
-        qt = buf[4 + b, 0]
-        s_diag = jnp.dot(knat[4 + b], qt, preferred_element_type=F32)
-        has_far = jnp.logical_or(step < 4, row > 0)
-        s_far = jnp.dot(knat[b], qt, preferred_element_type=F32)
-        s = jnp.where(causal, s_diag, jnp.where(has_far, s_far, NEG))
-        m = jnp.max(s, axis=0, keepdims=True)
-        p = jnp.exp2((s - m) * scale)
-        l = jnp.sum(p, axis=0, keepdims=True)
-        p_diag = jnp.where(causal, p, 0.0).astype(BF16)
-        acc = jnp.dot(buf[4 + b, 2], p_diag, preferred_element_type=F32)
-        p_far = jnp.where(causal, 0.0, p).astype(BF16)
-        v_far = jnp.where(has_far, buf[b, 2], jnp.zeros((hd, tok), BF16))
-        acc = acc + jnp.dot(v_far, p_far, preferred_element_type=F32)
-
-        def mid(j, carry):
-            m, l, acc = carry
-            s = jnp.dot(knat[j], qt, preferred_element_type=F32)
-            m_new = jnp.maximum(m, jnp.max(s, axis=0, keepdims=True))
-            alpha = jnp.exp2((m - m_new) * scale)
-            p = jnp.exp2((s - m_new) * scale)
-            l = alpha * l + jnp.sum(p, axis=0, keepdims=True)
-            acc = alpha * acc + jnp.dot(buf[j, 2], p.astype(BF16), preferred_element_type=F32)
-            return m_new, l, acc
-
-        first = jnp.where(row > 0, b + 1, jnp.maximum(b + 1, 4))
-        m, l, acc = lax.fori_loop(first, b + 4, mid, (m, l, acc))
-        osend[b] = (acc / l).astype(BF16)
-
-        @pl.when(b != g)
-        def _():
-            out_copy(b).start()
-        return 0
-
-    def out_copy(b):
-        return pltpu.make_async_remote_copy(
-            src_ref=osend.at[b],
-            dst_ref=oland.at[g],
-            send_sem=osend_sem.at[b],
-            recv_sem=orecv_sem.at[g],
-            device_id=at_group(b), device_id_type=MESH)
-
-    @pl.when(row == 0)
-    def _():
-        for i in range(4):
-            knat[i] = jnp.zeros((tok, hd), BF16)
-    lax.fori_loop(0, 8, one_block, 0)
-    oland[g] = osend[g]
-    for b in range(8):
-        @pl.when(b != g)
-        def _(b=b):
-            pltpu.make_async_copy(oland.at[b], oland.at[b], orecv_sem.at[b]).wait()
-    out_ref[...] = oland[...].reshape(8 * hd, tok).T
-    for d in range(1, 8):
-        block_copy(d).wait_send()
-    for b in range(8):
-        @pl.when(b != g)
-        def _(b=b):
-            out_copy(b).wait_send()
-
-    @pl.when(row < 7)
-    def _():
-        for i in range(4):
-            halo_copy(i).wait_send()
-
-
-def attention(proj):
-    V = pltpu.VMEM
-    D = pltpu.SemaphoreType.DMA
-    return pl.pallas_call(
-        attn_kernel,
-        name="attn",
-        out_shape=jax.ShapeDtypeStruct((512, 768), BF16),
-        in_specs=[pl.BlockSpec(memory_space=V)],
-        out_specs=pl.BlockSpec(memory_space=V),
-        scratch_shapes=[
-            V((3, 768, 512), BF16), V((12, 3, 96, 512), BF16), V((12, 512, 96), BF16),
-            V((8, 96, 512), BF16), V((8, 96, 512), BF16),
-            D((8,)), D((8,)), D((4,)), D((4,)), D((8,)), D((8,)),
-        ],
-        compiler_params=pltpu.CompilerParams(
-            collective_id=3, has_side_effects=True, vmem_limit_bytes=56 * 2**20),
-    )(proj)
 
 def parts_of(v, count):
     out = []
@@ -481,6 +281,241 @@
             collective_id=1, has_side_effects=True, vmem_limit_bytes=60 * 2**20),
     )(x, b, c, step.T, ld.T, skip.reshape(1, 24), hg.reshape(1, wid))
 
+def back_kernel(n_ref, res_ref, wo_hbm, wq_hbm, gain_ref, stream_ref, out_ref,
+                wo_p, wo_o, wq, base, psend, precv, srecv,
+                own, buf, knat, osend, oland,
+                w_sem, p_send, p_recv, s_send, s_recv,
+                send_sem, recv_sem, hsend_sem, hrecv_sem, osend_sem, orecv_sem):
+    z = lax.axis_index("seq_0")
+    yh = lax.axis_index("seq_1")
+    xx = lax.axis_index("seq_2")
+    cc = lax.axis_index("seq_3")
+    tp = lax.axis_index("tp")
+    g = xx * 2 + cc
+    row = z * 2 + yh
+    nrow = lax.rem(row + 1, 8)
+    prow = lax.rem(row + 7, 8)
+    hd, tok, ch, nch, half = 96, 512, 128, 4, 1536
+
+    def at_group(j):
+        return {"seq_2": j // 2, "seq_3": lax.rem(j, 2)}
+
+    def at_row(r):
+        return {"seq_0": r // 2, "seq_1": lax.rem(r, 2)}
+
+    partner = {"tp": 1 - tp}
+    own_cols = pl.ds(pl.multiple_of(tp * half, half), half)
+    far_cols = pl.ds(pl.multiple_of((1 - tp) * half, half), half)
+
+    def dot(a, b):
+        return jnp.dot(a, b, preferred_element_type=F32)
+
+    loads = [
+        pltpu.make_async_copy(wo_hbm.at[:, far_cols], wo_p, w_sem.at[0]),
+        pltpu.make_async_copy(wo_hbm.at[:, own_cols], wo_o, w_sem.at[1]),
+        pltpu.make_async_copy(wq_hbm, wq, w_sem.at[2]),
+    ]
+    for load in loads:
+        load.start()
+
+    barrier = pltpu.get_barrier_semaphore()
+    for d in range(1, 8):
+        pl.semaphore_signal(barrier, inc=1, device_id=at_group(lax.rem(g + d, 8)), device_id_type=MESH)
+    for dev in (at_row(nrow), at_row(prow), partner):
+        pl.semaphore_signal(barrier, inc=1, device_id=dev, device_id_type=MESH)
+    pl.semaphore_wait(barrier, 10)
+
+    def rows(c):
+        return slice(c * ch, (c + 1) * ch)
+
+    def p_copy(c):
+        return pltpu.make_async_remote_copy(
+            src_ref=psend.at[c], dst_ref=precv.at[c], send_sem=p_send.at[c],
+            recv_sem=p_recv.at[c], device_id=partner, device_id_type=MESH)
+
+    def s_copy(c):
+        return pltpu.make_async_remote_copy(
+            src_ref=stream_ref.at[pl.ds(c * ch, ch)], dst_ref=srecv.at[c], send_sem=s_send.at[c],
+            recv_sem=s_recv.at[c], device_id=partner, device_id_type=MESH)
+
+    loads[0].wait()
+    for c in range(nch):
+        psend[c] = dot(n_ref[rows(c)], wo_p[...]).astype(BF16)
+        p_copy(c).start()
+    loads[1].wait()
+    for c in range(nch):
+        base[rows(c)] = res_ref[rows(c)].astype(F32) + dot(n_ref[rows(c)], wo_o[...])
+    for c in range(nch):
+        p_copy(c).wait_recv()
+        stream_ref[rows(c)] = (base[rows(c)] + precv[c].astype(F32)).astype(BF16)
+        s_copy(c).start()
+    loads[2].wait()
+
+    def head(j):
+        return pl.ds(pl.multiple_of(j * hd, 32), hd)
+
+    def block_copy(c, d):
+        j = lax.rem(g + d, 8)
+        return pltpu.make_async_remote_copy(
+            src_ref=own.at[c, :, head(j), :],
+            dst_ref=buf.at[4 + g, c],
+            send_sem=send_sem.at[c, d],
+            recv_sem=recv_sem.at[c, g],
+            device_id=at_group(j), device_id_type=MESH)
+
+    def halo_copy(c, i):
+        return pltpu.make_async_remote_copy(
+            src_ref=buf.at[8 + i, c, pl.ds(1, 2)],
+            dst_ref=buf.at[i, c, pl.ds(1, 2)],
+            send_sem=hsend_sem.at[c, i],
+            recv_sem=hrecv_sem.at[c, i],
+            device_id=at_row(nrow), device_id_type=MESH)
+
+    def out_copy(b):
+        return pltpu.make_async_remote_copy(
+            src_ref=osend.at[b],
+            dst_ref=oland.at[g],
+            send_sem=osend_sem.at[b],
+            recv_sem=orecv_sem.at[g],
+            device_id=at_group(b), device_id_type=MESH)
+
+    def landed(ref, sem):
+        pltpu.make_async_copy(ref, ref, sem).wait()
+
+    def arrivals(c):
+        for b in (4, 5, 6, 7, 0, 1, 2, 3):
+            @pl.when(b != g)
+            def _(b=b):
+                landed(buf.at[4 + b, c], recv_sem.at[c, b])
+            if b >= 4:
+                @pl.when(row < 7)
+                def _(b=b):
+                    halo_copy(c, b - 4).start()
+        for b in range(8):
+            knat[4 + b, c * ch:(c + 1) * ch, :] = buf[4 + b, c, 1].T
+
+    gain_own = gain_ref[0:1, own_cols]
+    gain_far = gain_ref[0:1, far_cols]
+    for c in range(nch):
+        landed(srecv.at[c], s_recv.at[c])
+        a = stream_ref[rows(c)].astype(F32)
+        f = srecv[c].astype(F32)
+        ss = jnp.sum(a * a, axis=1, keepdims=True) + jnp.sum(f * f, axis=1, keepdims=True)
+        inv = lax.rsqrt(ss * (1.0 / (2 * half)) + EPSILON)
+        na = (a * inv * gain_own).astype(BF16)
+        nf = (f * inv * gain_far).astype(BF16)
+        for i in range(3):
+            r = dot(na, wq[i, own_cols, :]) + dot(nf, wq[i, far_cols, :])
+            own[c, i] = r.astype(BF16).T
+        for d in (4, 5, 3, 2, 6, 1, 7):
+            block_copy(c, d).start()
+        buf[4 + g, c] = own[c, :, head(g), :]
+        if c > 0:
+            arrivals(c - 1)
+    arrivals(nch - 1)
+
+    scale = (hd ** -0.5) * LOG2E
+    spos = lax.broadcasted_iota(jnp.int32, (tok, tok), 0)
+    tpos = lax.broadcasted_iota(jnp.int32, (tok, tok), 1)
+    causal = spos <= tpos
+
+    def wide(j, i):
+        return jnp.concatenate([buf[j, c, i] for c in range(nch)], axis=1)
+
+    @pl.when(row == 0)
+    def _():
+        for i in range(4):
+            knat[i] = jnp.zeros((tok, hd), BF16)
+
+    def one_block(step, _):
+        b = jnp.where(step < 4, 4 + step, 7 - step)
+
+        @pl.when(jnp.logical_and(step >= 4, row > 0))
+        def _():
+            for c in range(nch):
+                halo_copy(c, b).wait_recv()
+                knat[b, c * ch:(c + 1) * ch, :] = buf[b, c, 1].T
+
+        qt = wide(4 + b, 0)
+        has_far = jnp.logical_or(step < 4, row > 0)
+        s_diag = dot(knat[4 + b], qt)
+        s_far = dot(knat[b], qt)
+        s = jnp.where(causal, s_diag, jnp.where(has_far, s_far, NEG))
+        m = jnp.max(s, axis=0, keepdims=True)
+        p = jnp.exp2((s - m) * scale)
+        l = jnp.sum(p, axis=0, keepdims=True)
+        p_diag = jnp.where(causal, p, 0.0).astype(BF16)
+        acc = dot(wide(4 + b, 2), p_diag)
+        p_far = jnp.where(causal, 0.0, p).astype(BF16)
+        v_far = jnp.where(has_far, wide(b, 2), jnp.zeros((hd, tok), BF16))
+        acc = acc + dot(v_far, p_far)
+
+        def mid(j, carry):
+            m, l, acc = carry
+            s = dot(knat[j], qt)
+            m_new = jnp.maximum(m, jnp.max(s, axis=0, keepdims=True))
+            alpha = jnp.exp2((m - m_new) * scale)
+            p = jnp.exp2((s - m_new) * scale)
+            l = alpha * l + jnp.sum(p, axis=0, keepdims=True)
+            acc = alpha * acc + dot(wide(j, 2), p.astype(BF16))
+            return m_new, l, acc
+
+        first = jnp.where(row > 0, b + 1, jnp.maximum(b + 1, 4))
+        m, l, acc = lax.fori_loop(first, b + 4, mid, (m, l, acc))
+        osend[b] = (acc / l).astype(BF16)
+
+        @pl.when(b != g)
+        def _():
+            out_copy(b).start()
+        return 0
+
+    lax.fori_loop(0, 8, one_block, 0)
+    oland[g] = osend[g]
+    for b in range(8):
+        @pl.when(b != g)
+        def _(b=b):
+            landed(oland.at[b], orecv_sem.at[b])
+    out_ref[...] = oland[...].reshape(8 * hd, tok).T
+    for c in range(nch):
+        p_copy(c).wait_send()
+        s_copy(c).wait_send()
+        for d in range(1, 8):
+            block_copy(c, d).wait_send()
+    for b in range(8):
+        @pl.when(b != g)
+        def _(b=b):
+            out_copy(b).wait_send()
+
+    @pl.when(row < 7)
+    def _():
+        for c in range(nch):
+            for i in range(4):
+                halo_copy(c, i).wait_send()
+
+
+def back(normed, residual, mixer_out, weight, gain):
+    V = pltpu.VMEM
+    D = pltpu.SemaphoreType.DMA
+    vm = pl.BlockSpec(memory_space=V)
+    hbm = pl.BlockSpec(memory_space=pl.ANY)
+    return pl.pallas_call(
+        back_kernel,
+        name="back",
+        out_shape=(jax.ShapeDtypeStruct((512, 1536), BF16), jax.ShapeDtypeStruct((512, 768), BF16)),
+        in_specs=[vm, vm, hbm, hbm, vm],
+        out_specs=(vm, vm),
+        scratch_shapes=[
+            V((1536, 1536), BF16), V((1536, 1536), BF16), V((3, 3072, 768), BF16),
+            V((512, 1536), F32), V((4, 128, 1536), BF16), V((4, 128, 1536), BF16), V((4, 128, 1536), BF16),
+            V((4, 3, 768, 128), BF16), V((12, 4, 3, 96, 128), BF16), V((12, 512, 96), BF16),
+            V((8, 96, 512), BF16), V((8, 96, 512), BF16),
+            D((3,)), D((4,)), D((4,)), D((4,)), D((4,)),
+            D((4, 8)), D((4, 8)), D((4, 4)), D((4, 4)), D((8,)), D((8,)),
+        ],
+        compiler_params=pltpu.CompilerParams(
+            collective_id=2, has_side_effects=True, vmem_limit_bytes=63 * 2**20),
+    )(normed, residual, mixer_out, weight, gain.reshape(1, 3072))
+
 
 def on_device(
     mixer_input,
@@ -495,31 +530,9 @@
     attn_gain,
     qkv_weight,
 ):
-    tokens_dev = mixer_input.shape[0]
-    head_count = step_size.shape[1]
-    channels = mixer_input.shape[1]
-    head_dim = channels // head_count
     normed = mixer(mixer_input, state_write, state_read, step_size, log_decay, skip_gain, head_gain)
-    partial_value = jnp.dot(normed, mixer_out, preferred_element_type=jnp.float32)
-    model_width = partial_value.shape[1]
-    half_width = residual.shape[1]
-    own_sum = sum_at_owner(partial_value.astype(jnp.bfloat16), "tp", 1)
-    stream = (residual.astype(jnp.float32) + own_sum).astype(jnp.bfloat16)
-    stream_wide = stream.astype(jnp.float32)
-    squares = over_copies(jnp.sum(stream_wide * stream_wide, axis=1), "tp")
-    gain_half = lax.dynamic_slice_in_dim(
-        attn_gain, lax.axis_index("tp") * half_width, half_width, 0
-    )
-    normed_half = (
-        stream_wide * lax.rsqrt(squares / model_width + EPSILON)[:, None] * gain_half
-    ).astype(jnp.bfloat16)
-    normed_stream = gathered_copies(normed_half, "tp", 1)
     weight = jnp.transpose(qkv_weight, (1, 0, 2))
-    projected = jnp.concatenate(
-        [jnp.dot(normed_stream, weight[i], preferred_element_type=jnp.float32).astype(jnp.bfloat16) for i in range(3)],
-        axis=1,
-    )
-    pieces = attention(projected)
+    stream, pieces = back(normed, residual, mixer_out, weight, attn_gain)
     return (stream, pieces)
 
 

time: 208 us -> 157 us (0.75)
  blocking collectives: 76.4 us -> 0 us
  Pallas kernels: 95.3 us -> 149 us
  matrix products: 18.7 us -> 0 us
  waiting for transfers between devices: 3.68 us -> 0 us
  starting transfers between devices: 3.22 us -> 0 us
  other arithmetic: 3.11 us -> 0 us
    all_to_all x2 -> x0, blocking collectives: 76.4 us -> none  [the longest x1 39.1 us: sum_at_owner(): lax.all_to_all(pieces, axis, split_axis=0, concat_axis=0, tiled=True)]
    pallas_call x1, Pallas kernels: 64.4 us -> 119 us  [back(): pl.pallas_call(back_kernel, name='back', out_shape=(jax.ShapeDtypeStruct(...]
    dot_general x4 -> x0, matrix products: 18.7 us -> none  [the longest x3 10.6 us: on_device(): jnp.dot(normed_stream, weight[i], preferred_element_type=jnp.float32)]
    all_to_all x1 -> x0, waiting for transfers between devices: 3.68 us -> none  [from_everyone(): lax.all_to_all(jnp.broadcast_to(x[None], (size, *x.shape)), axis, 0, 0, t...]
    all_to_all x1 -> x0, starting transfers between devices: 3.22 us -> none  [from_everyone(): lax.all_to_all(jnp.broadcast_to(x[None], (size, *x.shape)), axis, 0, 0, t...]
  transfers between devices with their start and end apart: 1 -> 0, of which waited for: 1 -> 0; matrix products, arithmetic and copies ran while one was open for 0% -> 0% of each run, Pallas kernels for 0% -> 0%
where the time goes in v3:
time: 157 us; the launch traced here: 155 us
  Pallas kernels  149 us (95%)
  local copies, waits for them, and re-layouts  4.9 us (3%)
    pallas_call x1, Pallas kernels, back(): pl.pallas_call(back_kernel, name='back', out_shape=(jax.ShapeDtypeStruct(...  119 us
    pallas_call x1, Pallas kernels, mixer(): pl.pallas_call(mixer_kernel, name='mixer', out_shape=jax.ShapeDtypeStruct...  30.9 us
    unnamed x4, local copies, waits for them, and re-layouts  3.61 us

profile of v3, /device:TPU:32, one launch (start us, length us, event | category | flops | bytes accessed | tf_op | source)
XLA Modules:
  0.0 155.0 jit_solution(3741293086458569990)
XLA Ops:
  0.6 1.3 reshape.14.hg_ref
  1.9 30.9 %mixer.1.n_ref = bf16[512,1536]{1,0:T(8,128)(2,1)} custom-call(bf16[512,1536]{1,0:T(8,128)(2,1)} %x_ref.1, bf16[512,128]{1,0:T(8,128)(2,1)} %b_ref.1, bf16[512,128]{1,0:T(8,128)(2,1)} %c_ref.1, f32[24,512]{1,0:T(8,128)} %bitcast.6, f32[24,512]{1,0:T(8,128)} %bitcast.7, f32[1,24]{1,0:T(1,128)} %bitcast.9, f32[1,1536]{1,0:T(1,128)} %reshape.14.hg_ref), custom_call_target="tpu_custom_call" | custom-call | tf_op jit(solution)/shard_map/mixer/pallas_call | solution.py:267
  32.9 118.6 %back.1 = (bf16[512,1536]{1,0:T(8,128)(2,1)}, bf16[512,768]{1,0:T(8,128)(2,1)}) custom-call(bf16[512,1536]{1,0:T(8,128)(2,1)} %mixer.1.n_ref, bf16[512,1536]{1,0:T(8,128)(2,1)} %res_ref.1, bf16[1536,3072]{1,0:T(8,128)(2,1)} %wo_hbm.1, bf16[3,3072,768]{2,1,0:T(8,128)(2,1)} %bitcast.5, f32[1,3072]{1,0:T(1,128)} %bitcast.8), custom_call_target="tpu_custom_call" | custom-call | tf_op jit(solution)/shard_map/back/pallas_call | solution.py:501
  151.4 0.0 copy-start
  151.4 2.7 %copy.15 = bf16[512,1536]{1,0:T(8,128)(2,1)} copy(bf16[512,1536]{1,0:T(8,128)(2,1)} %get-tuple-element.4) | data formatting | bytes 3145728
  154.2 0.0 copy-done
  154.2 0.9 copy.16
Async XLA Ops:
  151.4 2.7 %copy-start = (bf16[512,768]{1,0:T(8,128)(2,1)S(1)}, bf16[512,768]{1,0:T(8,128)(2,1)}, u32[]{:S(2)}) copy-start(bf16[512,768]{1,0:T(8,128)(2,1)} %get-tuple-element.5) | copy-start | bytes 2359300

commit v4 on v3

--- a/solution.py
+++ b/solution.py
@@ -89,9 +89,6 @@
     step_col = step_ref[...].T
     w_col = jnp.concatenate(wt, axis=1).T
     e_col = jnp.exp2(g_col)
-    eexp[...] = expand(e_col)
-    one3 = one_hot((3 * nh, nh * 128), 128, nh)
-    gexp[...] = dot(jnp.concatenate(parts_of(g_col, 3), axis=1), one3)
     state = None
     for c in range(2):
         rows = slice(c * blk, (c + 1) * blk)
@@ -102,7 +99,7 @@
         if c == 0:
             s0[...] = term
         else:
-            state = eexp[2 * blk - 1:2 * blk] * s0[...] + term
+            state = expand(e_col[2 * blk - 8:2 * blk])[7:8] * s0[...] + term
     stage[...] = state.astype(BF16)
     pl.semaphore_wait(barrier, 14)
 
@@ -150,6 +147,9 @@
         a_copy(d).start()
     rs[g] = stage[slice_of(g), :]
     tr[g] = tst[...]
+    one3 = one_hot((3 * nh, nh * 128), 128, nh)
+    gexp[...] = dot(jnp.concatenate(parts_of(g_col, 3), axis=1), one3)
+    eexp[...] = expand(e_col)
 
     causal = si >= ti
 
@@ -247,7 +247,7 @@
         sq = parts_of(y * y, 2)
         ssum = dot(sq[0], et) + dot(sq[1], et)
         inv = lax.rsqrt(ssum * (1.0 / 64.0) + EPSILON)
-        n_ref[rows] = (y * expand(inv) * hg_ref[...]).astype(BF16)
+        n_ref[rows] = (y * expand(inv) * hg_ref[...].reshape(1, wid)).astype(BF16)
 
     for d in range(1, 8):
         at_copy(d).wait_send()
@@ -279,11 +279,11 @@
         ] + [D((8,))] * 10,
         compiler_params=pltpu.CompilerParams(
             collective_id=1, has_side_effects=True, vmem_limit_bytes=60 * 2**20),
-    )(x, b, c, step.T, ld.T, skip.reshape(1, 24), hg.reshape(1, wid))
+    )(x, b, c, step.T, ld.T, skip.reshape(1, 24), hg)
 
 def back_kernel(n_ref, res_ref, wo_hbm, wq_hbm, gain_ref, stream_ref, out_ref,
                 wo_p, wo_o, wq, base, psend, precv, srecv,
-                own, buf, knat, osend, oland,
+                own, buf, knat, osend, oland, mkeep, lkeep, akeep,
                 w_sem, p_send, p_recv, s_send, s_recv,
                 send_sem, recv_sem, hsend_sem, hrecv_sem, osend_sem, orecv_sem):
     z = lax.axis_index("seq_0")
@@ -394,8 +394,8 @@
         for b in range(8):
             knat[4 + b, c * ch:(c + 1) * ch, :] = buf[4 + b, c, 1].T
 
-    gain_own = gain_ref[0:1, own_cols]
-    gain_far = gain_ref[0:1, far_cols]
+    gain_own = gain_ref[own_cols].reshape(1, half)
+    gain_far = gain_ref[far_cols].reshape(1, half)
     for c in range(nch):
         landed(srecv.at[c], s_recv.at[c])
         a = stream_ref[rows(c)].astype(F32)
@@ -412,64 +412,119 @@
         buf[4 + g, c] = own[c, :, head(g), :]
         if c > 0:
             arrivals(c - 1)
-    arrivals(nch - 1)
-
     scale = (hd ** -0.5) * LOG2E
-    spos = lax.broadcasted_iota(jnp.int32, (tok, tok), 0)
-    tpos = lax.broadcasted_iota(jnp.int32, (tok, tok), 1)
-    causal = spos <= tpos
-
-    def wide(j, i):
-        return jnp.concatenate([buf[j, c, i] for c in range(nch)], axis=1)
+    early = 3 * ch
+
+    def causal(n):
+        return (lax.broadcasted_iota(jnp.int32, (n, n), 0)
+                <= lax.broadcasted_iota(jnp.int32, (n, n), 1))
+
+    def wide(j, i, lo, hi):
+        return jnp.concatenate([buf[j, c, i] for c in range(lo, hi)], axis=1)
 
     @pl.when(row == 0)
     def _():
         for i in range(4):
             knat[i] = jnp.zeros((tok, hd), BF16)
-
-    def one_block(step, _):
-        b = jnp.where(step < 4, 4 + step, 7 - step)
-
+            for c in range(nch):
+                buf[i, c, 2] = jnp.zeros((hd, ch), BF16)
+
+    def order(step):
+        return jnp.where(step < 4, 4 + step, 7 - step)
+
+    def halo_in(step, b, lo, hi):
         @pl.when(jnp.logical_and(step >= 4, row > 0))
         def _():
-            for c in range(nch):
+            for c in range(lo, hi):
                 halo_copy(c, b).wait_recv()
                 knat[b, c * ch:(c + 1) * ch, :] = buf[b, c, 1].T
 
-        qt = wide(4 + b, 0)
+    low = causal(early)
+
+    def first_round(step, _):
+        b = order(step)
+        halo_in(step, b, 0, 3)
+        qt = wide(4 + b, 0, 0, 3)
         has_far = jnp.logical_or(step < 4, row > 0)
-        s_diag = dot(knat[4 + b], qt)
-        s_far = dot(knat[b], qt)
-        s = jnp.where(causal, s_diag, jnp.where(has_far, s_far, NEG))
+        s_diag = dot(knat[4 + b, 0:early], qt)
+        s_far = dot(knat[b, 0:early], qt)
+        s = jnp.where(low, s_diag, jnp.where(has_far, s_far, NEG))
         m = jnp.max(s, axis=0, keepdims=True)
         p = jnp.exp2((s - m) * scale)
         l = jnp.sum(p, axis=0, keepdims=True)
-        p_diag = jnp.where(causal, p, 0.0).astype(BF16)
-        acc = dot(wide(4 + b, 2), p_diag)
-        p_far = jnp.where(causal, 0.0, p).astype(BF16)
-        v_far = jnp.where(has_far, wide(b, 2), jnp.zeros((hd, tok), BF16))
-        acc = acc + dot(v_far, p_far)
+        acc = dot(wide(4 + b, 2, 0, 3), jnp.where(low, p, 0.0).astype(BF16))
+        acc = acc + dot(wide(b, 2, 0, 3), jnp.where(low, 0.0, p).astype(BF16))
 
         def mid(j, carry):
             m, l, acc = carry
-            s = dot(knat[j], qt)
+            s = dot(knat[j, 0:early], qt)
             m_new = jnp.maximum(m, jnp.max(s, axis=0, keepdims=True))
             alpha = jnp.exp2((m - m_new) * scale)
             p = jnp.exp2((s - m_new) * scale)
             l = alpha * l + jnp.sum(p, axis=0, keepdims=True)
-            acc = alpha * acc + dot(wide(j, 2), p.astype(BF16))
+            acc = alpha * acc + dot(wide(j, 2, 0, 3), p.astype(BF16))
             return m_new, l, acc
 
         first = jnp.where(row > 0, b + 1, jnp.maximum(b + 1, 4))
         m, l, acc = lax.fori_loop(first, b + 4, mid, (m, l, acc))
-        osend[b] = (acc / l).astype(BF16)
+        mkeep[b] = m
+        lkeep[b] = l
+        akeep[b] = acc
+        return 0
+
+    lax.fori_loop(0, 8, first_round, 0)
+    arrivals(nch - 1)
+    low1 = causal(ch)
+
+    def second_round(step, _):
+        b = order(step)
+        halo_in(step, b, 3, 4)
+
+        def there(i):
+            return jnp.logical_or(b + i >= 4, row > 0)
+
+        qt = wide(4 + b, 0, 0, 3)
+        ss = [jnp.where(there(i), dot(knat[b + i, early:tok], qt), NEG) for i in range(4)]
+        m = mkeep[b]
+        m_new = m
+        for t in ss:
+            m_new = jnp.maximum(m_new, jnp.max(t, axis=0, keepdims=True))
+        alpha = jnp.exp2((m - m_new) * scale)
+        ps = [jnp.exp2((t - m_new) * scale) for t in ss]
+        l = alpha * lkeep[b]
+        for t in ps:
+            l = l + jnp.sum(t, axis=0, keepdims=True)
+        pt = jnp.concatenate([t.astype(BF16) for t in ps], axis=0)
+        vt = jnp.concatenate([buf[b + i, 3, 2] for i in range(4)], axis=1)
+        acc = alpha * akeep[b] + dot(vt, pt)
+        osend[b, :, 0:early] = (acc / l).astype(BF16)
+
+        qt = buf[4 + b, 3, 0]
+        s_diag = dot(knat[4 + b, early:tok], qt)
+        s_far = dot(knat[b, early:tok], qt)
+        ss = [jnp.where(low1, s_diag, jnp.where(there(0), s_far, NEG)), dot(knat[4 + b, 0:early], qt)]
+        ss += [jnp.where(there(i), dot(knat[b + i], qt), NEG) for i in range(1, 4)]
+        m = jnp.max(ss[0], axis=0, keepdims=True)
+        for t in ss[1:]:
+            m = jnp.maximum(m, jnp.max(t, axis=0, keepdims=True))
+        ps = [jnp.exp2((t - m) * scale) for t in ss]
+        l = jnp.sum(ps[0], axis=0, keepdims=True)
+        for t in ps[1:]:
+            l = l + jnp.sum(t, axis=0, keepdims=True)
+        pt = jnp.concatenate(
+            [jnp.where(low1, ps[0], 0.0).astype(BF16), jnp.where(low1, 0.0, ps[0]).astype(BF16)]
+            + [t.astype(BF16) for t in ps[1:]], axis=0)
+        vt = jnp.concatenate(
+            [buf[4 + b, 3, 2], buf[b, 3, 2], wide(4 + b, 2, 0, 3)]
+            + [wide(b + i, 2, 0, 4) for i in range(1, 4)], axis=1)
+        osend[b, :, early:tok] = (dot(vt, pt) / l).astype(BF16)
 
         @pl.when(b != g)
         def _():
             out_copy(b).start()
         return 0
 
-    lax.fori_loop(0, 8, one_block, 0)
+    lax.fori_loop(0, 8, second_round, 0)
     oland[g] = osend[g]
     for b in range(8):
         @pl.when(b != g)
@@ -509,12 +564,13 @@
             V((512, 1536), F32), V((4, 128, 1536), BF16), V((4, 128, 1536), BF16), V((4, 128, 1536), BF16),
             V((4, 3, 768, 128), BF16), V((12, 4, 3, 96, 128), BF16), V((12, 512, 96), BF16),
             V((8, 96, 512), BF16), V((8, 96, 512), BF16),
+            V((8, 1, 384), F32), V((8, 1, 384), F32), V((8, 96, 384), F32),
             D((3,)), D((4,)), D((4,)), D((4,)), D((4,)),
             D((4, 8)), D((4, 8)), D((4, 4)), D((4, 4)), D((8,)), D((8,)),
         ],
         compiler_params=pltpu.CompilerParams(
             collective_id=2, has_side_effects=True, vmem_limit_bytes=63 * 2**20),
-    )(normed, residual, mixer_out, weight, gain.reshape(1, 3072))
+    )(normed, residual, mixer_out, weight, gain)
 
 
 def on_device(

time: 157 us -> 156 us (level); the launches traced: 155 us -> 156 us
  Pallas kernels: 149 us -> 152 us
    pallas_call x1, Pallas kernels: 119 us -> 121 us  [back(): pl.pallas_call(back_kernel, name='back', out_shape=(jax.ShapeDtypeStruct(...]
where the time goes in v4:
time: 156 us
  Pallas kernels  152 us (97%)
  local copies, waits for them, and re-layouts  3.61 us (2%)
    pallas_call x1, Pallas kernels, back(): pl.pallas_call(back_kernel, name='back', out_shape=(jax.ShapeDtypeStruct(...  121 us
    pallas_call x1, Pallas kernels, mixer(): pl.pallas_call(mixer_kernel, name='mixer', out_shape=jax.ShapeDtypeStruct...  31.1 us
    unnamed x4, local copies, waits for them, and re-layouts  3.61 us

profile of v4, /device:TPU:32, one launch (start us, length us, event | category | flops | bytes accessed | tf_op | source)
XLA Modules:
  0.0 156.1 jit_solution(2561601599766889245)
XLA Ops:
  0.6 31.1 %mixer.1.n_ref = bf16[512,1536]{1,0:T(8,128)(2,1)} custom-call(bf16[512,1536]{1,0:T(8,128)(2,1)} %x_ref.1, bf16[512,128]{1,0:T(8,128)(2,1)} %b_ref.1, bf16[512,128]{1,0:T(8,128)(2,1)} %c_ref.1, f32[24,512]{1,0:T(8,128)} %bitcast.5, f32[24,512]{1,0:T(8,128)} %bitcast.6, f32[1,24]{1,0:T(1,128)} %bitcast.7, f32[1536]{0:T(1024)} %hg_ref.1), custom_call_target="tpu_custom_call" | custom-call | tf_op jit(solution)/shard_map/mixer/pallas_call | solution.py:267
  31.7 120.7 %back.1 = (bf16[512,1536]{1,0:T(8,128)(2,1)}, bf16[512,768]{1,0:T(8,128)(2,1)}) custom-call(bf16[512,1536]{1,0:T(8,128)(2,1)} %mixer.1.n_ref, bf16[512,1536]{1,0:T(8,128)(2,1)} %res_ref.1, bf16[1536,3072]{1,0:T(8,128)(2,1)} %wo_hbm.1, bf16[3,3072,768]{2,1,0:T(8,128)(2,1)} %bitcast.4, f32[3072]{0:T(1024)} %gain_ref.1), custom_call_target="tpu_custom_call" | custom-call | tf_op jit(solution)/shard_map/back/pallas_call | solution.py:556
  152.4 0.0 copy-start
  152.4 2.7 %copy.15 = bf16[512,1536]{1,0:T(8,128)(2,1)} copy(bf16[512,1536]{1,0:T(8,128)(2,1)} %get-tuple-element.4) | data formatting | bytes 3145728
  155.2 0.0 copy-done
  155.2 0.9 copy.16
Async XLA Ops:
  152.4 2.7 %copy-start = (bf16[512,768]{1,0:T(8,128)(2,1)S(1)}, bf16[512,768]{1,0:T(8,128)(2,1)}, u32[]{:S(2)}) copy-start(bf16[512,768]{1,0:T(8,128)(2,1)} %get-tuple-element.5) | copy-start | bytes 2359300

commit v5 on v4

--- a/solution.py
+++ b/solution.py
@@ -285,7 +285,7 @@
                 wo_p, wo_o, wq, base, psend, precv, srecv,
                 own, buf, knat, osend, oland, mkeep, lkeep, akeep,
                 w_sem, p_send, p_recv, s_send, s_recv,
-                send_sem, recv_sem, hsend_sem, hrecv_sem, osend_sem, orecv_sem):
+                send_sem, recv_sem, qsend_sem, qrecv_sem, hsend_sem, hrecv_sem, osend_sem, orecv_sem):
     z = lax.axis_index("seq_0")
     yh = lax.axis_index("seq_1")
     xx = lax.axis_index("seq_2")
@@ -323,8 +323,6 @@
         pl.semaphore_signal(barrier, inc=1, device_id=at_group(lax.rem(g + d, 8)), device_id_type=MESH)
     for dev in (at_row(nrow), at_row(prow), partner):
         pl.semaphore_signal(barrier, inc=1, device_id=dev, device_id_type=MESH)
-    pl.semaphore_wait(barrier, 10)
-
     def rows(c):
         return slice(c * ch, (c + 1) * ch)
 
@@ -338,29 +336,49 @@
             src_ref=stream_ref.at[pl.ds(c * ch, ch)], dst_ref=srecv.at[c], send_sem=s_send.at[c],
             recv_sem=s_recv.at[c], device_id=partner, device_id_type=MESH)
 
+    def project(c):
+        psend[c] = dot(n_ref[rows(c)], wo_p[...]).astype(BF16)
+
+    def add_up(c):
+        p_copy(c).wait_recv()
+        stream_ref[rows(c)] = (base[rows(c)] + precv[c].astype(F32)).astype(BF16)
+        s_copy(c).start()
+
     loads[0].wait()
-    for c in range(nch):
-        psend[c] = dot(n_ref[rows(c)], wo_p[...]).astype(BF16)
-        p_copy(c).start()
+    project(0)
+    pl.semaphore_wait(barrier, 10)
+    p_copy(0).start()
+    project(1)
+    p_copy(1).start()
     loads[1].wait()
     for c in range(nch):
         base[rows(c)] = res_ref[rows(c)].astype(F32) + dot(n_ref[rows(c)], wo_o[...])
-    for c in range(nch):
-        p_copy(c).wait_recv()
-        stream_ref[rows(c)] = (base[rows(c)] + precv[c].astype(F32)).astype(BF16)
-        s_copy(c).start()
+    project(2)
+    project(3)
+    for c in range(2):
+        add_up(c)
+        p_copy(c + 2).start()
     loads[2].wait()
 
     def head(j):
         return pl.ds(pl.multiple_of(j * hd, 32), hd)
 
-    def block_copy(c, d):
+    def kv_copy(c, d):
         j = lax.rem(g + d, 8)
         return pltpu.make_async_remote_copy(
-            src_ref=own.at[c, :, head(j), :],
-            dst_ref=buf.at[4 + g, c],
+            src_ref=own.at[c, pl.ds(1, 2), head(j), :],
+            dst_ref=buf.at[4 + g, c, pl.ds(1, 2)],
             send_sem=send_sem.at[c, d],
             recv_sem=recv_sem.at[c, g],
+            device_id=at_group(j), device_id_type=MESH)
+
+    def q_copy(c, d):
+        j = lax.rem(g + d, 8)
+        return pltpu.make_async_remote_copy(
+            src_ref=own.at[c, 0, head(j), :],
+            dst_ref=buf.at[4 + g, c, 0],
+            send_sem=qsend_sem.at[c, d],
+            recv_sem=qrecv_sem.at[c, g],
             device_id=at_group(j), device_id_type=MESH)
 
     def halo_copy(c, i):
@@ -386,13 +404,17 @@
         for b in (4, 5, 6, 7, 0, 1, 2, 3):
             @pl.when(b != g)
             def _(b=b):
-                landed(buf.at[4 + b, c], recv_sem.at[c, b])
+                landed(buf.at[4 + b, c, pl.ds(1, 2)], recv_sem.at[c, b])
             if b >= 4:
                 @pl.when(row < 7)
                 def _(b=b):
                     halo_copy(c, b - 4).start()
         for b in range(8):
             knat[4 + b, c * ch:(c + 1) * ch, :] = buf[4 + b, c, 1].T
+        for b in range(8):
+            @pl.when(b != g)
+            def _(b=b):
+                landed(buf.at[4 + b, c, 0], qrecv_sem.at[c, b])
 
     gain_own = gain_ref[own_cols].reshape(1, half)
     gain_far = gain_ref[far_cols].reshape(1, half)
@@ -404,12 +426,17 @@
         inv = lax.rsqrt(ss * (1.0 / (2 * half)) + EPSILON)
         na = (a * inv * gain_own).astype(BF16)
         nf = (f * inv * gain_far).astype(BF16)
-        for i in range(3):
+        for i in (1, 2, 0):
             r = dot(na, wq[i, own_cols, :]) + dot(nf, wq[i, far_cols, :])
             own[c, i] = r.astype(BF16).T
-        for d in (4, 5, 3, 2, 6, 1, 7):
-            block_copy(c, d).start()
+            for d in (4, 5, 3, 2, 6, 1, 7):
+                if i == 2:
+                    kv_copy(c, d).start()
+                if i == 0:
+                    q_copy(c, d).start()
         buf[4 + g, c] = own[c, :, head(g), :]
+        if c < 2:
+            add_up(c + 2)
         if c > 0:
             arrivals(c - 1)
     scale = (hd ** -0.5) * LOG2E
@@ -535,7 +562,8 @@
         p_copy(c).wait_send()
         s_copy(c).wait_send()
         for d in range(1, 8):
-            block_copy(c, d).wait_send()
+            kv_copy(c, d).wait_send()
+            q_copy(c, d).wait_send()
     for b in range(8):
         @pl.when(b != g)
         def _(b=b):
@@ -566,10 +594,10 @@
             V((8, 96, 512), BF16), V((8, 96, 512), BF16),
             V((8, 1, 384), F32), V((8, 1, 384), F32), V((8, 96, 384), F32),
             D((3,)), D((4,)), D((4,)), D((4,)), D((4,)),
-            D((4, 8)), D((4, 8)), D((4, 4)), D((4, 4)), D((8,)), D((8,)),
+            D((4, 8)), D((4, 8)), D((4, 8)), D((4, 8)), D((4, 4)), D((4, 4)), D((8,)), D((8,)),
         ],
         compiler_params=pltpu.CompilerParams(
-            collective_id=2, has_side_effects=True, vmem_limit_bytes=63 * 2**20),
+            collective_id=2, has_side_effects=True, vmem_limit_bytes=54 * 2**20),
     )(normed, residual, mixer_out, weight, gain)
 
 

time: 156 us -> 156 us (level)
  no operation moved by 1% of the time
where the time goes in v5:
time: 156 us
  Pallas kernels  152 us (97%)
  local copies, waits for them, and re-layouts  3.61 us (2%)
    pallas_call x1, Pallas kernels, back(): pl.pallas_call(back_kernel, name='back', out_shape=(jax.ShapeDtypeStruct(...  121 us
    pallas_call x1, Pallas kernels, mixer(): pl.pallas_call(mixer_kernel, name='mixer', out_shape=jax.ShapeDtypeStruct...  31.1 us
    unnamed x4, local copies, waits for them, and re-layouts  3.61 us

profile of v5, /device:TPU:32, one launch (start us, length us, event | category | flops | bytes accessed | tf_op | source)
XLA Modules:
  0.0 155.9 jit_solution(1629941572498671696)
XLA Ops:
  0.6 31.1 %mixer.1.n_ref = bf16[512,1536]{1,0:T(8,128)(2,1)} custom-call(bf16[512,1536]{1,0:T(8,128)(2,1)} %x_ref.1, bf16[512,128]{1,0:T(8,128)(2,1)} %b_ref.1, bf16[512,128]{1,0:T(8,128)(2,1)} %c_ref.1, f32[24,512]{1,0:T(8,128)} %bitcast.5, f32[24,512]{1,0:T(8,128)} %bitcast.6, f32[1,24]{1,0:T(1,128)} %bitcast.7, f32[1536]{0:T(1024)} %hg_ref.1), custom_call_target="tpu_custom_call" | custom-call | tf_op jit(solution)/shard_map/mixer/pallas_call | solution.py:267
  31.7 120.6 %back.1 = (bf16[512,1536]{1,0:T(8,128)(2,1)}, bf16[512,768]{1,0:T(8,128)(2,1)}) custom-call(bf16[512,1536]{1,0:T(8,128)(2,1)} %mixer.1.n_ref, bf16[512,1536]{1,0:T(8,128)(2,1)} %res_ref.1, bf16[1536,3072]{1,0:T(8,128)(2,1)} %wo_hbm.1, bf16[3,3072,768]{2,1,0:T(8,128)(2,1)} %bitcast.4, f32[3072]{0:T(1024)} %gain_ref.1), custom_call_target="tpu_custom_call" | custom-call | tf_op jit(solution)/shard_map/back/pallas_call | solution.py:584
  152.3 0.0 copy-start
  152.3 2.7 %copy.15 = bf16[512,1536]{1,0:T(8,128)(2,1)} copy(bf16[512,1536]{1,0:T(8,128)(2,1)} %get-tuple-element.4) | data formatting | bytes 3145728
  155.0 0.0 copy-done
  155.0 0.9 copy.16
Async XLA Ops:
  152.3 2.7 %copy-start = (bf16[512,768]{1,0:T(8,128)(2,1)S(1)}, bf16[512,768]{1,0:T(8,128)(2,1)}, u32[]{:S(2)}) copy-start(bf16[512,768]{1,0:T(8,128)(2,1)} %get-tuple-element.5) | copy-start | bytes 2359300

commit v6 on v5

--- a/solution.py
+++ b/solution.py
@@ -416,6 +416,103 @@
             def _(b=b):
                 landed(buf.at[4 + b, c, 0], qrecv_sem.at[c, b])
 
+    scale = (hd ** -0.5) * LOG2E
+    early = 2 * ch
+    low = (lax.broadcasted_iota(jnp.int32, (early, early), 0)
+           <= lax.broadcasted_iota(jnp.int32, (early, early), 1))
+
+    def wide(j, i, lo, hi):
+        return jnp.concatenate([buf[j, c, i] for c in range(lo, hi)], axis=1)
+
+    @pl.when(row == 0)
+    def _():
+        for i in range(4):
+            knat[i] = jnp.zeros((tok, hd), BF16)
+            for c in range(nch):
+                buf[i, c, 2] = jnp.zeros((hd, ch), BF16)
+
+    def order(step):
+        return jnp.where(step < 4, 4 + step, 7 - step)
+
+    def halo_in(step, b, lo, hi):
+        @pl.when(jnp.logical_and(step >= 4, row > 0))
+        def _():
+            for c in range(lo, hi):
+                halo_copy(c, b).wait_recv()
+                knat[b, c * ch:(c + 1) * ch, :] = buf[b, c, 1].T
+
+    def top(tiles):
+        m = None
+        for t, ok in tiles:
+            r = jnp.max(t, axis=0, keepdims=True)
+            if ok is not None:
+                r = jnp.where(ok, r, NEG)
+            m = r if m is None else jnp.maximum(m, r)
+        return m
+
+    def powers(tiles, m):
+        ps = [jnp.exp2(t - (m if ok is None else jnp.where(ok, m, -NEG))) for t, ok in tiles]
+        l = jnp.sum(ps[0], axis=0, keepdims=True)
+        for t in ps[1:]:
+            l = l + jnp.sum(t, axis=0, keepdims=True)
+        return ps, l
+
+    def square(b, lo, hi, qt, far):
+        s_diag = dot(knat[4 + b, lo:hi], qt)
+        s_far = dot(knat[b, lo:hi], qt)
+        return jnp.where(low, s_diag, jnp.where(far, s_far, NEG))
+
+    def halves(p):
+        return [jnp.where(low, p, 0.0).astype(BF16), jnp.where(low, 0.0, p).astype(BF16)]
+
+    def there(b, i):
+        return jnp.logical_or(b + i >= 4, row > 0)
+
+    def first_round(step, _):
+        b = order(step)
+        halo_in(step, b, 0, 2)
+        qt = wide(4 + b, 0, 0, 2)
+        tiles = [(square(b, 0, early, qt, there(b, 0)), None)]
+        tiles += [(dot(knat[b + i, 0:early], qt), there(b, i)) for i in range(1, 4)]
+        m = top(tiles)
+        ps, l = powers(tiles, m)
+        pt = jnp.concatenate(halves(ps[0]) + [t.astype(BF16) for t in ps[1:]], axis=0)
+        vt = jnp.concatenate([wide(j, 2, 0, 2) for j in (4 + b, b, b + 1, b + 2, b + 3)], axis=1)
+        mkeep[b] = m
+        lkeep[b] = l
+        akeep[b] = dot(vt, pt)
+        return 0
+
+    def second_round(step, _):
+        b = order(step)
+        halo_in(step, b, 2, 4)
+
+        qt = wide(4 + b, 0, 0, 2)
+        tiles = [(dot(knat[b + i, early:tok], qt), there(b, i)) for i in range(4)]
+        m = mkeep[b]
+        m_new = jnp.maximum(m, top(tiles))
+        alpha = jnp.exp2(m - m_new)
+        ps, l = powers(tiles, m_new)
+        l = alpha * lkeep[b] + l
+        pt = jnp.concatenate([t.astype(BF16) for t in ps], axis=0)
+        vt = jnp.concatenate([wide(b + i, 2, 2, 4) for i in range(4)], axis=1)
+        osend[b, :, 0:early] = ((alpha * akeep[b] + dot(vt, pt)) / l).astype(BF16)
+
+        qt = wide(4 + b, 0, 2, 4)
+        tiles = [(square(b, early, tok, qt, there(b, 0)), None), (dot(knat[4 + b, 0:early], qt), None)]
+        tiles += [(dot(knat[b + i], qt), there(b, i)) for i in range(1, 4)]
+        ps, l = powers(tiles, top(tiles))
+        pt = jnp.concatenate(halves(ps[0]) + [t.astype(BF16) for t in ps[1:]], axis=0)
+        vt = jnp.concatenate(
+            [wide(4 + b, 2, 2, 4), wide(b, 2, 2, 4), wide(4 + b, 2, 0, 2)]
+            + [wide(b + i, 2, 0, 4) for i in range(1, 4)], axis=1)
+        osend[b, :, early:tok] = (dot(vt, pt) / l).astype(BF16)
+
+        @pl.when(b != g)
+        def _():
+            out_copy(b).start()
+        return 0
+
     gain_own = gain_ref[own_cols].reshape(1, half)
     gain_far = gain_ref[far_cols].reshape(1, half)
     for c in range(nch):
@@ -428,6 +525,8 @@
         nf = (f * inv * gain_far).astype(BF16)
         for i in (1, 2, 0):
             r = dot(na, wq[i, own_cols, :]) + dot(nf, wq[i, far_cols, :])
+            if i == 0:
+                r = r * scale
             own[c, i] = r.astype(BF16).T
             for d in (4, 5, 3, 2, 6, 1, 7):
                 if i == 2:
@@ -439,118 +538,9 @@
             add_up(c + 2)
         if c > 0:
             arrivals(c - 1)
-    scale = (hd ** -0.5) * LOG2E
-    early = 3 * ch
-
-    def causal(n):
-        return (lax.broadcasted_iota(jnp.int32, (n, n), 0)
-                <= lax.broadcasted_iota(jnp.int32, (n, n), 1))
-
-    def wide(j, i, lo, hi):
-        return jnp.concatenate([buf[j, c, i] for c in range(lo, hi)], axis=1)
-
-    @pl.when(row == 0)
-    def _():
-        for i in range(4):
-            knat[i] = jnp.zeros((tok, hd), BF16)
-            for c in range(nch):
-                buf[i, c, 2] = jnp.zeros((hd, ch), BF16)
-
-    def order(step):
-        return jnp.where(step < 4, 4 + step, 7 - step)
-
-    def halo_in(step, b, lo, hi):
-        @pl.when(jnp.logical_and(step >= 4, row > 0))
-        def _():
-            for c in range(lo, hi):
-                halo_copy(c, b).wait_recv()
-                knat[b, c * ch:(c + 1) * ch, :] = buf[b, c, 1].T
-
-    low = causal(early)
-
-    def first_round(step, _):
-        b = order(step)
-        halo_in(step, b, 0, 3)
-        qt = wide(4 + b, 0, 0, 3)
-        has_far = jnp.logical_or(step < 4, row > 0)
-        s_diag = dot(knat[4 + b, 0:early], qt)
-        s_far = dot(knat[b, 0:early], qt)
-        s = jnp.where(low, s_diag, jnp.where(has_far, s_far, NEG))
-        m = jnp.max(s, axis=0, keepdims=True)
-        p = jnp.exp2((s - m) * scale)
-        l = jnp.sum(p, axis=0, keepdims=True)
-        acc = dot(wide(4 + b, 2, 0, 3), jnp.where(low, p, 0.0).astype(BF16))
-        acc = acc + dot(wide(b, 2, 0, 3), jnp.where(low, 0.0, p).astype(BF16))
-
-        def mid(j, carry):
-            m, l, acc = carry
-            s = dot(knat[j, 0:early], qt)
-            m_new = jnp.maximum(m, jnp.max(s, axis=0, keepdims=True))
-            alpha = jnp.exp2((m - m_new) * scale)
-            p = jnp.exp2((s - m_new) * scale)
-            l = alpha * l + jnp.sum(p, axis=0, keepdims=True)
-            acc = alpha * acc + dot(wide(j, 2, 0, 3), p.astype(BF16))
-            return m_new, l, acc
-
-        first = jnp.where(row > 0, b + 1, jnp.maximum(b + 1, 4))
-        m, l, acc = lax.fori_loop(first, b + 4, mid, (m, l, acc))
-        mkeep[b] = m
-        lkeep[b] = l
-        akeep[b] = acc
-        return 0
-
-    lax.fori_loop(0, 8, first_round, 0)
+        if c == 2:
+            lax.fori_loop(0, 8, first_round, 0)
     arrivals(nch - 1)
-    low1 = causal(ch)
-
-    def second_round(step, _):
-        b = order(step)
-        halo_in(step, b, 3, 4)
-
-        def there(i):
-            return jnp.logical_or(b + i >= 4, row > 0)
-
-        qt = wide(4 + b, 0, 0, 3)
-        ss = [jnp.where(there(i), dot(knat[b + i, early:tok], qt), NEG) for i in range(4)]
-        m = mkeep[b]
-        m_new = m
-        for t in ss:
-            m_new = jnp.maximum(m_new, jnp.max(t, axis=0, keepdims=True))
-        alpha = jnp.exp2((m - m_new) * scale)
-        ps = [jnp.exp2((t - m_new) * scale) for t in ss]
-        l = alpha * lkeep[b]
-        for t in ps:
-            l = l + jnp.sum(t, axis=0, keepdims=True)
-        pt = jnp.concatenate([t.astype(BF16) for t in ps], axis=0)
-        vt = jnp.concatenate([buf[b + i, 3, 2] for i in range(4)], axis=1)
-        acc = alpha * akeep[b] + dot(vt, pt)
-        osend[b, :, 0:early] = (acc / l).astype(BF16)
-
-        qt = buf[4 + b, 3, 0]
-        s_diag = dot(knat[4 + b, early:tok], qt)
-        s_far = dot(knat[b, early:tok], qt)
-        ss = [jnp.where(low1, s_diag, jnp.where(there(0), s_far, NEG)), dot(knat[4 + b, 0:early], qt)]
-        ss += [jnp.where(there(i), dot(knat[b + i], qt), NEG) for i in range(1, 4)]
-        m = jnp.max(ss[0], axis=0, keepdims=True)
-        for t in ss[1:]:
-            m = jnp.maximum(m, jnp.max(t, axis=0, keepdims=True))
-        ps = [jnp.exp2((t - m) * scale) for t in ss]
-        l = jnp.sum(ps[0], axis=0, keepdims=True)
-        for t in ps[1:]:
-            l = l + jnp.sum(t, axis=0, keepdims=True)
-        pt = jnp.concatenate(
-            [jnp.where(low1, ps[0], 0.0).astype(BF16), jnp.where(low1, 0.0, ps[0]).astype(BF16)]
-            + [t.astype(BF16) for t in ps[1:]], axis=0)
-        vt = jnp.concatenate(
-            [buf[4 + b, 3, 2], buf[b, 3, 2], wide(4 + b, 2, 0, 3)]
-            + [wide(b + i, 2, 0, 4) for i in range(1, 4)], axis=1)
-        osend[b, :, early:tok] = (dot(vt, pt) / l).astype(BF16)
-
-        @pl.when(b != g)
-        def _():
-            out_copy(b).start()
-        return 0
-
     lax.fori_loop(0, 8, second_round, 0)
     oland[g] = osend[g]
     for b in range(8):
@@ -592,7 +582,7 @@
             V((512, 1536), F32), V((4, 128, 1536), BF16), V((4, 128, 1536), BF16), V((4, 128, 1536), BF16),
             V((4, 3, 768, 128), BF16), V((12, 4, 3, 96, 128), BF16), V((12, 512, 96), BF16),
             V((8, 96, 512), BF16), V((8, 96, 512), BF16),
-            V((8, 1, 384), F32), V((8, 1, 384), F32), V((8, 96, 384), F32),
+            V((8, 1, 256), F32), V((8, 1, 256), F32), V((8, 96, 256), F32),
             D((3,)), D((4,)), D((4,)), D((4,)), D((4,)),
             D((4, 8)), D((4, 8)), D((4, 8)), D((4, 8)), D((4, 4)), D((4, 4)), D((8,)), D((8,)),
         ],

time: 156 us -> 159 us (1.019); the launches traced: 156 us -> 157 us
  no operation moved by 1% of the time
where the time goes in v6:
time: 159 us; the launch traced here: 157 us
  Pallas kernels  153 us (96%)
  local copies, waits for them, and re-layouts  3.61 us (2%)
    pallas_call x1, Pallas kernels, back(): pl.pallas_call(back_kernel, name='back', out_shape=(jax.ShapeDtypeStruct(...  122 us
    pallas_call x1, Pallas kernels, mixer(): pl.pallas_call(mixer_kernel, name='mixer', out_shape=jax.ShapeDtypeStruct...  31.1 us
    unnamed x4, local copies, waits for them, and re-layouts  3.61 us

profile of v6, /device:TPU:32, one launch (start us, length us, event | category | flops | bytes accessed | tf_op | source)
XLA Modules:
  0.0 157.1 jit_solution(15273566828542350698)
XLA Ops:
  0.6 31.1 %mixer.1.n_ref = bf16[512,1536]{1,0:T(8,128)(2,1)} custom-call(bf16[512,1536]{1,0:T(8,128)(2,1)} %x_ref.1, bf16[512,128]{1,0:T(8,128)(2,1)} %b_ref.1, bf16[512,128]{1,0:T(8,128)(2,1)} %c_ref.1, f32[24,512]{1,0:T(8,128)} %bitcast.5, f32[24,512]{1,0:T(8,128)} %bitcast.6, f32[1,24]{1,0:T(1,128)} %bitcast.7, f32[1536]{0:T(1024)} %hg_ref.1), custom_call_target="tpu_custom_call" | custom-call | tf_op jit(solution)/shard_map/mixer/pallas_call | solution.py:267
  31.7 121.8 %back.1 = (bf16[512,1536]{1,0:T(8,128)(2,1)}, bf16[512,768]{1,0:T(8,128)(2,1)}) custom-call(bf16[512,1536]{1,0:T(8,128)(2,1)} %mixer.1.n_ref, bf16[512,1536]{1,0:T(8,128)(2,1)} %res_ref.1, bf16[1536,3072]{1,0:T(8,128)(2,1)} %wo_hbm.1, bf16[3,3072,768]{2,1,0:T(8,128)(2,1)} %bitcast.4, f32[3072]{0:T(1024)} %gain_ref.1), custom_call_target="tpu_custom_call" | custom-call | tf_op jit(solution)/shard_map/back/pallas_call | solution.py:574
  153.5 0.0 copy-start
  153.5 2.7 %copy.15 = bf16[512,1536]{1,0:T(8,128)(2,1)} copy(bf16[512,1536]{1,0:T(8,128)(2,1)} %get-tuple-element.4) | data formatting | bytes 3145728
  156.2 0.0 copy-done
  156.2 0.9 copy.16
Async XLA Ops:
  153.5 2.7 %copy-start = (bf16[512,768]{1,0:T(8,128)(2,1)S(1)}, bf16[512,768]{1,0:T(8,128)(2,1)}, u32[]{:S(2)}) copy-start(bf16[512,768]{1,0:T(8,128)(2,1)} %get-tuple-element.5) | copy-start | bytes 2359300

commit v7 on v6

--- a/solution.py
+++ b/solution.py
@@ -401,7 +401,7 @@
         pltpu.make_async_copy(ref, ref, sem).wait()
 
     def arrivals(c):
-        for b in (4, 5, 6, 7, 0, 1, 2, 3):
+        for b in (7, 6, 5, 4, 0, 1, 2, 3):
             @pl.when(b != g)
             def _(b=b):
                 landed(buf.at[4 + b, c, pl.ds(1, 2)], recv_sem.at[c, b])
@@ -539,7 +539,9 @@
         if c > 0:
             arrivals(c - 1)
         if c == 2:
-            lax.fori_loop(0, 8, first_round, 0)
+            lax.fori_loop(0, 4, first_round, 0)
+        if c == 3:
+            lax.fori_loop(4, 8, first_round, 0)
     arrivals(nch - 1)
     lax.fori_loop(0, 8, second_round, 0)
     oland[g] = osend[g]

time: 159 us -> 147 us (0.925)
  Pallas kernels: 153 us -> 140 us
    pallas_call x1, Pallas kernels: 122 us -> 109 us  [back(): pl.pallas_call(back_kernel, name='back', out_shape=(jax.ShapeDtypeStruct(...]
where the time goes in v7:
time: 147 us; the launch traced here: 145 us
  Pallas kernels  140 us (95%)
  local copies, waits for them, and re-layouts  3.61 us (2%)
    pallas_call x1, Pallas kernels, back(): pl.pallas_call(back_kernel, name='back', out_shape=(jax.ShapeDtypeStruct(...  109 us
    pallas_call x1, Pallas kernels, mixer(): pl.pallas_call(mixer_kernel, name='mixer', out_shape=jax.ShapeDtypeStruct...  31.1 us
    unnamed x4, local copies, waits for them, and re-layouts  3.61 us

profile of v7, /device:TPU:32, one launch (start us, length us, event | category | flops | bytes accessed | tf_op | source)
XLA Modules:
  0.0 144.7 jit_solution(2200279665787662377)
XLA Ops:
  0.6 31.1 %mixer.1.n_ref = bf16[512,1536]{1,0:T(8,128)(2,1)} custom-call(bf16[512,1536]{1,0:T(8,128)(2,1)} %x_ref.1, bf16[512,128]{1,0:T(8,128)(2,1)} %b_ref.1, bf16[512,128]{1,0:T(8,128)(2,1)} %c_ref.1, f32[24,512]{1,0:T(8,128)} %bitcast.5, f32[24,512]{1,0:T(8,128)} %bitcast.6, f32[1,24]{1,0:T(1,128)} %bitcast.7, f32[1536]{0:T(1024)} %hg_ref.1), custom_call_target="tpu_custom_call" | custom-call | tf_op jit(solution)/shard_map/mixer/pallas_call | solution.py:267
  31.7 109.4 %back.1 = (bf16[512,1536]{1,0:T(8,128)(2,1)}, bf16[512,768]{1,0:T(8,128)(2,1)}) custom-call(bf16[512,1536]{1,0:T(8,128)(2,1)} %mixer.1.n_ref, bf16[512,1536]{1,0:T(8,128)(2,1)} %res_ref.1, bf16[1536,3072]{1,0:T(8,128)(2,1)} %wo_hbm.1, bf16[3,3072,768]{2,1,0:T(8,128)(2,1)} %bitcast.4, f32[3072]{0:T(1024)} %gain_ref.1), custom_call_target="tpu_custom_call" | custom-call | tf_op jit(solution)/shard_map/back/pallas_call | solution.py:576
  141.1 0.0 copy-start
  141.1 2.7 %copy.15 = bf16[512,1536]{1,0:T(8,128)(2,1)} copy(bf16[512,1536]{1,0:T(8,128)(2,1)} %get-tuple-element.4) | data formatting | bytes 3145728
  143.8 0.0 copy-done
  143.9 0.9 copy.16
Async XLA Ops:
  141.1 2.7 %copy-start = (bf16[512,768]{1,0:T(8,128)(2,1)S(1)}, bf16[512,768]{1,0:T(8,128)(2,1)}, u32[]{:S(2)}) copy-start(bf16[512,768]{1,0:T(8,128)(2,1)} %get-tuple-element.5) | copy-start | bytes 2359300
